TPU v7x, 512 devices: a whole 4x8x8 slice. The times are simulated.
512 devices in a mesh: group: 16 (over y, core), dom: 32 (over x, z).
Axes of the slice: x: 4, y: 8, z: 8, core: 2. Of those that a mesh axis runs over, the one named last changes fastest.
Arguments:
- hidden: bfloat16 [524288, 512], P(('group', 'dom')), may hold values from -6 to 6
- enc_weight: bfloat16 [512, 512], replicated, may hold values from -0.25 to 0.25
- enc_bias: float32 [512], replicated, may hold values from -3 to 3
- enc_slope: float32 [512], replicated, may hold values from 0.05 to 0.5
- dec_token: bfloat16 [512], replicated, may hold values from -4 to 4
- dec_weight: bfloat16 [512, 128], replicated, may hold values from -0.25 to 0.25
- dec_bias: float32 [128], replicated, may hold values from -3 to 3
- targets: bfloat16 [524288, 128], P(('group', 'dom')), may hold values from -6 to 6
- local_tiles: bfloat16 [6144, 128, 128], P(('group', 'dom')), may hold values from -0.375 to 0.375
- local_src: int32 [512, 12], P(('group', 'dom')), may hold values from 0 to 7
- local_dst: int32 [512, 12], P(('group', 'dom')), may hold values from 0 to 7
- local_count: int32 [512], P(('group', 'dom')), may hold values from 4 to 12, as said below
- halo_tiles: bfloat16 [4096, 128, 128], P(('group', 'dom')), may hold values from -0.375 to 0.375
- halo_src: int32 [512, 8], P(('group', 'dom')), may hold values from 0 to 7, each once within a row
- halo_dst: int32 [512, 8], P(('group', 'dom')), may hold values from 0 to 7
- send_rows: int32 [16384, 16], P(('group', 'dom')), may hold values from 0 to 1023
- cross_rows: int32 [8192, 32], P(('group', 'dom')), may hold values from 0 to 1023
- mask_nodes: int32 [512, 512], P(('group', 'dom')), may hold values from 0 to 1023, as said below
- remask_nodes: int32 [512, 256], P(('group', 'dom')), may hold values from 0 to 1023, as said below
Outputs:
- rebuilt: bfloat16 [524288, 128], P(('group', 'dom'))
- node_error: float32 [524288], P(('group', 'dom'))
Inputs may be any that keep to these rules, and one draw needn't show every extreme that they name: `local_count`: live local tiles of a partition; tile slots at or past it are ignored; some partition has 12. `halo_src`: each partition's row names each of its boundary blocks once. `mask_nodes`: distinct rows within a partition. `remask_nodes`: distinct rows within a partition.
All inputs are finite; a program needn't handle non-finite values.
Results may differ from a plain program's by a relative error of at most 0.0056.
Values may be sent and summed in bfloat16 or wider, within the bound.
A program may use at most 64 MiB of HBM per device.

v0:
```python
import jax
import jax.numpy as jnp
from jax import lax
from jax.sharding import PartitionSpec as P

BLK = 128


def project(inputs, weight):
    return jnp.dot(inputs, weight, preferred_element_type=jnp.float32).astype(jnp.bfloat16)


def spread(tile_values, sources, targets, live_tiles, source_pool, blocks):
    tile_count = tile_values.shape[0]
    block_rows = tile_values.shape[1]
    width = source_pool.shape[2]
    picked = source_pool[sources].reshape(tile_count * block_rows, width)
    side_by_side = jnp.transpose(tile_values, (1, 0, 2)).reshape(
        block_rows, tile_count * block_rows
    )
    tile_owner = jnp.repeat(targets, block_rows)
    column_live = jnp.repeat(live_tiles, block_rows)

    def one_block(target):
        keep = ((tile_owner == target) & column_live).astype(jnp.bfloat16)
        chosen = side_by_side * keep[None, :]
        return jnp.dot(chosen, picked, preferred_element_type=jnp.float32)

    summed = lax.map(one_block, jnp.arange(blocks, dtype=jnp.int32))
    return summed.reshape(blocks * block_rows, width)


def propagate(
    own_rows,
    halo_pool,
    local_tiles,
    local_src,
    local_dst,
    live_tiles,
    halo_tiles,
    halo_src,
    halo_dst,
):
    width = own_rows.shape[1]
    blocks = own_rows.shape[0] // BLK
    own_blocks = own_rows.reshape(blocks, BLK, width)
    remote_blocks = halo_pool.reshape(-1, BLK, width)
    every_tile = jnp.ones(halo_src.shape, jnp.bool_)
    inner = spread(local_tiles, local_src, local_dst, live_tiles, own_blocks, blocks)
    outer = spread(halo_tiles, halo_src, halo_dst, every_tile, remote_blocks, blocks)
    return inner + outer


def per_device(
    hidden,
    enc_weight,
    enc_bias,
    enc_slope,
    dec_token,
    dec_weight,
    dec_bias,
    targets,
    local_tiles,
    local_src,
    local_dst,
    local_count,
    halo_tiles,
    halo_src,
    halo_dst,
    send_rows,
    cross_rows,
    mask_nodes,
    remask_nodes,
):
    row_count = hidden.shape[0]
    width = hidden.shape[1]
    narrow_width = dec_weight.shape[1]
    source_blocks = local_src[0]
    target_blocks = local_dst[0]
    halo_sources = halo_src[0]
    halo_targets = halo_dst[0]
    live_tiles = jnp.arange(local_tiles.shape[0], dtype=jnp.int32) < local_count[0]
    encoded = project(hidden, enc_weight)
    dom_rows = lax.all_to_all(encoded[send_rows], "dom", split_axis=0, concat_axis=0, tiled=True)
    group_rows = lax.all_to_all(
        encoded[cross_rows], "group", split_axis=0, concat_axis=0, tiled=True
    )
    halo_pool = jnp.concatenate(
        [dom_rows.reshape(-1, width), group_rows.reshape(-1, width)], axis=0
    )
    summed = (
        propagate(
            encoded,
            halo_pool,
            local_tiles,
            source_blocks,
            target_blocks,
            live_tiles,
            halo_tiles,
            halo_sources,
            halo_targets,
        )
        + enc_bias[None, :]
    )
    latent = jnp.where(summed > 0, summed, enc_slope[None, :] * summed).astype(jnp.bfloat16)
    positions = jnp.arange(row_count, dtype=jnp.int32)
    remasked = jnp.any(remask_nodes[0][None, :] == positions[:, None], axis=1)
    masked = jnp.any(mask_nodes[0][None, :] == positions[:, None], axis=1)
    decoder_in = jnp.where(remasked[:, None], dec_token[None, :], latent)
    narrowed = project(decoder_in, dec_weight)
    dom_back = lax.all_to_all(narrowed[send_rows], "dom", split_axis=0, concat_axis=0, tiled=True)
    group_back = lax.all_to_all(
        narrowed[cross_rows], "group", split_axis=0, concat_axis=0, tiled=True
    )
    back_pool = jnp.concatenate(
        [dom_back.reshape(-1, narrow_width), group_back.reshape(-1, narrow_width)], axis=0
    )
    decoded = (
        propagate(
            narrowed,
            back_pool,
            local_tiles,
            source_blocks,
            target_blocks,
            live_tiles,
            halo_tiles,
            halo_sources,
            halo_targets,
        )
        + dec_bias[None, :]
    )
    rebuilt = decoded.astype(jnp.bfloat16)
    values = rebuilt.astype(jnp.float32)
    target_values = targets.astype(jnp.float32)
    cosine = (
        jnp.mean(values * target_values, axis=1)
        * lax.rsqrt(jnp.mean(values * values, axis=1) + 1e-06)
        * lax.rsqrt(jnp.mean(target_values * target_values, axis=1) + 1e-06)
    )
    node_error = jnp.where(masked, (1.0 - cosine) ** 2, jnp.zeros_like(cosine))
    return (rebuilt, node_error)


def solution(mesh):
    in_specs = (
        P(("group", "dom"), None),
        P(),
        P(),
        P(),
        P(),
        P(),
        P(),
        P(("group", "dom"), None),
        P(("group", "dom"), None, None),
        P(("group", "dom"), None),
        P(("group", "dom"), None),
        P(("group", "dom")),
        P(("group", "dom"), None, None),
        P(("group", "dom"), None),
        P(("group", "dom"), None),
        P(("group", "dom"), None),
        P(("group", "dom"), None),
        P(("group", "dom"), None),
        P(("group", "dom"), None),
    )
    out_specs = (P(("group", "dom"), None), P(("group", "dom")))
    return jax.shard_map(
        per_device, mesh=mesh, in_specs=in_specs, out_specs=out_specs, check_vma=False
    )
```

profile of v0, /device:TPU:1, one launch (start us, length us, event | category | flops | bytes accessed | tf_op | source)
XLA Modules:
  0.0 152.0 jit_solution(9395077613243013348)
XLA Ops:
  1.9 1.7 %convolution_convert_fusion = bf16[1024,512]{1,0:T(8,128)(2,1)S(1)} fusion(bf16[1024,512]{1,0:T(8,128)(2,1)S(1)} %copy-done, bf16[512,512]{1,0:T(8,128)(2,1)} %param.28), kind=kOutput, calls=%fused_computation.45 | convolution fusion | flops 537395200 | bytes 2621440 | tf_op jit(solution)/shard_map/dot_general | solution.py:10
  3.6 2.6 %gather_fusion.2 = bf16[512,512]{1,0:T(8,128)(2,1)} fusion(bf16[1024,512]{1,0:T(8,128)(2,1)S(1)} %convolution_convert_fusion, s32[1024]{0:T(1024)S(1)} %pad_clamp_fusion.1), kind=kCustom, calls=%fused_computation.2 | custom fusion | bytes 1050624 | tf_op jit(solution)/shard_map/gather | solution.py:86
  6.3 10.3 %all-to-all-start.1 = ((bf16[16,32,512]{2,1,0:T(8,128)(2,1)}), bf16[16,32,512]{2,1,0:T(8,128)(2,1)S(1)}, u32[]{:S(2)}, u32[]{:S(2)}) async-start(bf16[16,32,512]{2,1,0:T(8,128)(2,1)} %bitcast.13), calls=%async_computation.1 | async-start | bytes 1048576 | tf_op jit(solution)/shard_map/all_to_all | solution.py:85
  17.9 2.6 %gather_fusion.1 = bf16[512,512]{1,0:T(8,128)(2,1)} fusion(bf16[1024,512]{1,0:T(8,128)(2,1)S(1)} %convolution_convert_fusion, s32[1024]{0:T(1024)S(1)} %pad_clamp_fusion.2), kind=kCustom, calls=%fused_computation.1 | custom fusion | bytes 1050624 | tf_op jit(solution)/shard_map/gather | solution.py:84
  21.1 1.9 %gather_fusion = bf16[12,128,512]{2,1,0:T(8,128)(2,1)} fusion(bf16[8,128,512]{2,1,0:T(8,128)(2,1)S(1)} %bitcast.148, s32[1024]{0:T(1024)S(1)} %pad_clamp_fusion.3), kind=kCustom, calls=%fused_computation | custom fusion | bytes 3145776 | tf_op jit(solution)/shard_map/gather | solution.py:17
  23.0 10.9 %all-to-all-done.1 = bf16[16,32,512]{2,1,0:T(8,128)(2,1)S(1)} async-done(((bf16[16,32,512]{2,1,0:T(8,128)(2,1)}), bf16[16,32,512]{2,1,0:T(8,128)(2,1)S(1)}, u32[]{:S(2)}, u32[]{:S(2)}) %all-to-all-start.1) | async-done | bytes 524320 | tf_op jit(solution)/shard_map/all_to_all | solution.py:85
  33.9 11.3 %all-to-all-start = ((bf16[32,16,512]{2,1,0:T(8,128)(2,1)}), bf16[32,16,512]{2,1,0:T(8,128)(2,1)}, u32[]{:S(2)}, u32[]{:S(2)}) async-start(bf16[32,16,512]{2,1,0:T(8,128)(2,1)} %bitcast.11), calls=%async_computation | async-start | bytes 1048576 | tf_op jit(solution)/shard_map/all_to_all | solution.py:84
  45.7 1.6 %broadcast.102.clone = f32[8,128,512]{2,1,0:T(8,128)} broadcast(f32[]{:T(128)} %constant.12.clone.1), dimensions={} | broadcast | bytes 2097156 | tf_op jit(solution)/shard_map/broadcast.17
  47.4 23.9 %while.44 = (s32[]{:T(128)}, f32[8,128,512]{2,1,0:T(8,128)}, s32[8]{0:T(128)}, bf16[128,1536]{1,0:T(8,128)(2,1)S(1)}, bf16[1536,512]{1,0:T(8,128)(2,1)S(1)}, /*i...) while((s32[]{:T(128)}, f32[8,128,512]{2,1,0:T(8,128)}, s32[8]{0:T(128)}, ...), condition=%wide.region_2.3_spmd.clone, body=%wide.region_1.2_spmd.clone.sunk | while | flops 201527808 | bytes 2234541 | solution.py:29
  47.4 1.2 dynamic_slice.21
  50.3 1.2 dynamic_slice.21
  59.3 1.2 dynamic_slice.21
  73.9 2.1 %pad_maximum_fusion = bf16[1024,512]{1,0:T(8,128)(2,1)} fusion(bf16[512,512]{1,0:T(8,128)(2,1)S(1)} %bitcast.155, bf16[512,512]{1,0:T(8,128)(2,1)} %bitcast.12), kind=kLoop, calls=%fused_computation.48 | loop fusion | flops 2097152 | bytes 2097152 | tf_op jit(solution)/shard_map/concatenate | solution.py:88
  75.9 1.9 %gather_fusion.3 = bf16[8,128,512]{2,1,0:T(8,128)(2,1)S(1)} fusion(bf16[8,128,512]{2,1,0:T(8,128)(2,1)} %bitcast.154, s32[1024]{0:T(1024)S(1)} %pad_clamp_fusion), kind=kCustom, calls=%fused_computation.3 | custom fusion | bytes 2097184 | tf_op jit(solution)/shard_map/gather | solution.py:17
  77.8 1.6 %broadcast.102.clone.1 = f32[8,128,512]{2,1,0:T(8,128)} broadcast(f32[]{:T(128)} %constant.12.clone.1), dimensions={} | broadcast | bytes 2097156 | tf_op jit(solution)/shard_map/broadcast.17
  79.4 17.6 %while.45 = (s32[]{:T(128)}, f32[8,128,512]{2,1,0:T(8,128)}, s32[8]{0:T(128)S(1)}, bf16[128,1024]{1,0:T(8,128)(2,1)S(1)}, bf16[1024,512]{1,0:T(8,128)(2,1)S(1)}, /*index=5*/s32[8]{0:T(128)S(1)}, s32[]{:T(128)}) while((s32[]{:T(128)}, f32[8,128,512]{2,1,0:T(8,128)}, s32[8]{0:T(128)S(1)}, bf16[128,1024]{1,0:T(8,128)(2,1)S(1)}, ...), condition=%wide.region_4.5_spmd.clone, body=%wide.region_3.4_spmd.clone.sunk | while | flops 134350848 | bytes 1577097 | solution.py:29
  97.0 2.7 %add.87 = f32[8,128,512]{2,1,0:T(8,128)S(1)} add(f32[8,128,512]{2,1,0:T(8,128)} %get-tuple-element.140, f32[8,128,512]{2,1,0:T(8,128)} %get-tuple-element.141) | non-fusion elementwise | flops 524288 | bytes 6291456 | tf_op jit(solution)/shard_map/add | solution.py:51
  101.1 1.9 %gather_fusion.6 = bf16[512,128]{1,0:T(8,128)(2,1)} fusion(bf16[1024,128]{1,0:T(8,128)(2,1)S(1)} %convolution_convert_fusion.1, s32[1024]{0:T(1024)S(1)} %pad_clamp_fusion.1), kind=kCustom, calls=%fused_computation.6 | custom fusion | bytes 264192 | tf_op jit(solution)/shard_map/gather | solution.py:113
  103.0 3.4 %all-to-all-start.3 = ((bf16[16,32,128]{2,1,0:T(8,128)(2,1)}), bf16[16,32,128]{2,1,0:T(8,128)(2,1)S(1)}, u32[]{:S(2)}, u32[]{:S(2)}) async-start(bf16[16,32,128]{2,1,0:T(8,128)(2,1)} %bitcast.25), calls=%async_computation.3 | async-start | bytes 262144 | tf_op jit(solution)/shard_map/all_to_all | solution.py:112
  106.7 1.9 %gather_fusion.5 = bf16[512,128]{1,0:T(8,128)(2,1)} fusion(bf16[1024,128]{1,0:T(8,128)(2,1)S(1)} %convolution_convert_fusion.1, s32[1024]{0:T(1024)S(1)} %pad_clamp_fusion.2), kind=kCustom, calls=%fused_computation.5 | custom fusion | bytes 264192 | tf_op jit(solution)/shard_map/gather | solution.py:111
  109.4 5.7 %all-to-all-done.3 = bf16[16,32,128]{2,1,0:T(8,128)(2,1)S(1)} async-done(((bf16[16,32,128]{2,1,0:T(8,128)(2,1)}), bf16[16,32,128]{2,1,0:T(8,128)(2,1)S(1)}, u32[]{:S(2)}, u32[]{:S(2)}) %all-to-all-start.3) | async-done | bytes 131104 | tf_op jit(solution)/shard_map/all_to_all | solution.py:112
  115.1 9.5 %all-to-all-start.2 = ((bf16[32,16,128]{2,1,0:T(8,128)(2,1)}), bf16[32,16,128]{2,1,0:T(8,128)(2,1)S(1)}, u32[]{:S(2)}, u32[]{:S(2)}) async-start(bf16[32,16,128]{2,1,0:T(8,128)(2,1)} %bitcast.23), calls=%async_computation.2 | async-start | bytes 262144 | tf_op jit(solution)/shard_map/all_to_all | solution.py:111
  124.6 12.6 %while.46 = (s32[]{:T(128)}, f32[8,128,128]{2,1,0:T(8,128)S(1)}, s32[8]{0:T(128)S(1)}, bf16[128,1536]{1,0:T(8,128)(2,1)S(1)}, bf16[1536,128]{1,0:T(8,128)(2,1)S(...) while((s32[]{:T(128)}, f32[8,128,128]{2,1,0:T(8,128)S(1)}, s32[8]{0:T(128)S(1)}, ...), condition=%wide.region_6.7_spmd.clone, body=%wide.region_5.6_spmd.clone.sunk | while | flops 50532864 | bytes 859309 | solution.py:29
  138.0 12.3 %while.47 = (s32[]{:T(128)}, f32[8,128,128]{2,1,0:T(8,128)S(1)}, s32[8]{0:T(128)S(1)}, bf16[128,1024]{1,0:T(8,128)(2,1)S(1)}, bf16[1024,128]{1,0:T(8,128)(2,1)S(1)}, /*index=5*/s32[8]{0:T(128)S(1)}, s32[]{:T(128)}) while((s32[]{:T(128)}, f32[8,128,128]{2,1,0:T(8,128)S(1)}, s32[8]{0:T(128)S(1)}, bf16[128,1024]{1,0:T(8,128)(2,1)S(1)}, ...), condition=%wide.region_8.9_spmd.clone, body=%wide.region_7.8_spmd.clone.sunk | while | flops 33687552 | bytes 594057 | solution.py:29
  (156 shorter events, 72.6 us)
Async XLA Ops:
  0.6 1.2 copy-start
  3.6 13.0 %copy-start.2 = (bf16[12,128,128]{2,1,0:T(8,128)(2,1)S(1)}, bf16[12,128,128]{2,1,0:T(8,128)(2,1)}, u32[]{:S(2)}) copy-start(bf16[12,128,128]{2,1,0:T(8,128)(2,1)} %param.35) | copy-start | bytes 1179652
  6.3 11.4 %copy-start.7 = (s32[32,16]{0,1:T(8,128)S(1)}, s32[32,16]{0,1:T(8,128)}, u32[]{:S(2)}) copy-start(s32[32,16]{0,1:T(8,128)} %param.42) | copy-start | bytes 6148
  6.3 27.6 %all-to-all-start.1 = ((bf16[16,32,512]{2,1,0:T(8,128)(2,1)}), bf16[16,32,512]{2,1,0:T(8,128)(2,1)S(1)}, u32[]{:S(2)}, u32[]{:S(2)}) async-start(bf16[16,32,512]{2,1,0:T(8,128)(2,1)} %bitcast.13), calls=%async_computation.1 | async-start | bytes 1048576 | tf_op jit(solution)/shard_map/all_to_all | solution.py:85
  17.9 2.6 %copy-start.14 = (s32[1,12]{1,0:T(1,128)S(1)}, s32[1,12]{1,0:T(1,128)}, u32[]{:S(2)}) copy-start(s32[1,12]{1,0:T(1,128)} %param.36) | copy-start | bytes 148
  20.5 0.6 copy-start.8
  23.0 24.4 %copy-start.1 = (bf16[12,128,512]{2,1,0:T(8,128)(2,1)S(1)}, bf16[12,128,512]{2,1,0:T(8,128)(2,1)}, u32[]{:S(2)}) copy-start(bf16[12,128,512]{2,1,0:T(8,128)(2,1)} %gather_fusion) | copy-start | bytes 4718596
  23.0 24.4 %copy-start.6 = (s32[1,12]{1,0:T(1,128)S(1)}, s32[1,12]{1,0:T(1,128)}, u32[]{:S(2)}) copy-start(s32[1,12]{1,0:T(1,128)} %param.37) | copy-start | bytes 148
  33.9 39.9 %all-to-all-start = ((bf16[32,16,512]{2,1,0:T(8,128)(2,1)}), bf16[32,16,512]{2,1,0:T(8,128)(2,1)}, u32[]{:S(2)}, u32[]{:S(2)}) async-start(bf16[32,16,512]{2,1,0:T(8,128)(2,1)} %bitcast.11), calls=%async_computation | async-start | bytes 1048576 | tf_op jit(solution)/shard_map/all_to_all | solution.py:84
  75.9 3.5 %copy-start.5 = (s32[1,8]{1,0:T(1,128)S(1)}, s32[1,8]{1,0:T(1,128)}, u32[]{:S(2)}) copy-start(s32[1,8]{1,0:T(1,128)} %param.41) | copy-start | bytes 100
  97.0 2.8 %copy-start.10 = (f32[512]{0:T(512)S(1)}, f32[512]{0:T(512)}, u32[]{:S(2)}) copy-start(f32[512]{0:T(512)} %param.30) | copy-start | bytes 6148
  97.0 2.8 %copy-start.11 = (f32[512]{0:T(512)S(1)}, f32[512]{0:T(512)}, u32[]{:S(2)}) copy-start(f32[512]{0:T(512)} %param.29) | copy-start | bytes 6148
  97.0 2.8 %copy-start.12 = (bf16[512]{0:T(512)(128)(2,1)S(1)}, bf16[512]{0:T(512)(128)(2,1)}, u32[]{:S(2)}) copy-start(bf16[512]{0:T(512)(128)(2,1)} %param.31) | copy-start | bytes 3076
  99.7 0.9 copy-start.4
  100.6 5.8 %copy-start.13 = (s32[1,512]{1,0:T(1,128)S(1)}, s32[1,512]{1,0:T(1,128)}, u32[]{:S(2)}) copy-start(s32[1,512]{1,0:T(1,128)} %param.44) | copy-start | bytes 6148
  103.0 12.1 %all-to-all-start.3 = ((bf16[16,32,128]{2,1,0:T(8,128)(2,1)}), bf16[16,32,128]{2,1,0:T(8,128)(2,1)S(1)}, u32[]{:S(2)}, u32[]{:S(2)}) async-start(bf16[16,32,128]{2,1,0:T(8,128)(2,1)} %bitcast.25), calls=%async_computation.3 | async-start | bytes 262144 | tf_op jit(solution)/shard_map/all_to_all | solution.py:112
  115.1 22.2 %all-to-all-start.2 = ((bf16[32,16,128]{2,1,0:T(8,128)(2,1)}), bf16[32,16,128]{2,1,0:T(8,128)(2,1)S(1)}, u32[]{:S(2)}, u32[]{:S(2)}) async-start(bf16[32,16,128]{2,1,0:T(8,128)(2,1)} %bitcast.23), calls=%async_computation.2 | async-start | bytes 262144 | tf_op jit(solution)/shard_map/all_to_all | solution.py:111
  137.3 13.0 %copy-start.9 = (f32[128]{0:T(128)S(1)}, f32[128]{0:T(128)}, u32[]{:S(2)}) copy-start(f32[128]{0:T(128)} %param.33) | copy-start | bytes 1540
  138.0 12.6 %copy-start.3 = (bf16[1024,128]{1,0:T(8,128)(2,1)S(1)}, bf16[1024,128]{1,0:T(8,128)(2,1)}, u32[]{:S(2)}) copy-start(bf16[1024,128]{1,0:T(8,128)(2,1)} %param.34) | copy-start | bytes 786436
where the time goes:
time: 153 us; the launch traced here: 152 us
  local copies, waits for them, and re-layouts  44.6 us (29%)
  starting transfers between devices  34.6 us (23%)
  other arithmetic  31.3 us (20%)
  matrix products  22.9 us (15%)
  waiting for transfers between devices  16.6 us (11%)
  between operations  1.59 us (1%)
    dynamic_slice x32, local copies, waits for them, and re-layouts, spread(): summed = lax.map(one_block, jnp.arange(blocks, dtype=jnp.int32))  23.5 us
    convert_element_type x32, other arithmetic, one_block(): keep = ((tile_owner == target) & column_live).astype(jnp.bfloat16)  21.8 us
    dot_general x32, matrix products, one_block(): return jnp.dot(chosen, picked, preferred_element_type=jnp.float32)  20.7 us
    all_to_all x1, starting transfers between devices, per_device(): lax.all_to_all(encoded[send_rows], 'dom', split_axis=0, concat_axis=0, ti...  11.3 us
    all_to_all x1, waiting for transfers between devices, per_device(): lax.all_to_all(encoded[cross_rows], 'group', split_axis=0, concat_axis=0,...  10.9 us
    all_to_all x1, starting transfers between devices, per_device(): lax.all_to_all(encoded[cross_rows], 'group', split_axis=0, concat_axis=0,...  10.3 us
    all_to_all x1, starting transfers between devices, per_device(): lax.all_to_all(narrowed[send_rows], 'dom', split_axis=0, concat_axis=0, t...  9.5 us
    all_to_all x1, waiting for transfers between devices, per_device(): lax.all_to_all(narrowed[cross_rows], 'group', split_axis=0, concat_axis=0...  5.7 us
  transfers between devices with their start and end apart: 4, of which 2 were waited for; matrix products, arithmetic and copies ran while one was open for 32% of the time, Pallas kernels for 0%

commit v1 on v0

v1 whole, which is shorter than its diff:
```python
import jax
import jax.numpy as jnp
from jax import lax
from jax.experimental import pallas as pl
from jax.experimental.pallas import tpu as pltpu
from jax.sharding import PartitionSpec as P

BLK = 128
F32 = jnp.float32
BF16 = jnp.bfloat16
I32 = jnp.int32
Z_ORDER = (4, 3, 5, 2, 6, 1, 7, 0)
G_ORDER = (0, 1, 2, 3)


def iota(shape, axis):
    return lax.broadcasted_iota(I32, shape, axis)


def step_kernel(
    hidden,
    enc_weight,
    enc_bias,
    enc_slope,
    dec_token,
    dec_weight,
    dec_bias,
    targets,
    local_tiles,
    local_src,
    local_dst,
    local_count,
    halo_tiles,
    halo_src,
    halo_dst,
    send_index,
    mask_nodes,
    remask_nodes,
    rebuilt,
    node_error,
    hid_v,
    encw_v,
    decw_v,
    tgt_v,
    lt_v,
    ht_v,
    enc,
    onehot,
    out_wide,
    in_wide,
    acc,
    remasked,
    masked,
    narrowed,
    out_thin,
    in_thin,
    acc_thin,
    load_sem,
    send_wide,
    recv_wide,
    send_thin,
    recv_thin,
):
    mg = lax.axis_index("group")
    md = lax.axis_index("dom")
    mx = md // 8
    mz = md % 8
    mq = mg // 4

    barrier = pltpu.get_barrier_semaphore()

    def greet_dom(k, carry):
        pl.semaphore_signal(
            barrier, inc=1, device_id=(mg, (md + k) % 32), device_id_type=pl.DeviceIdType.MESH
        )
        return carry

    def greet_group(k, carry):
        pl.semaphore_signal(
            barrier, inc=1, device_id=((mg + k) % 16, md), device_id_type=pl.DeviceIdType.MESH
        )
        return carry

    lax.fori_loop(1, 32, greet_dom, 0)
    lax.fori_loop(1, 16, greet_group, 0)

    loads = [
        pltpu.make_async_copy(src, dst, load_sem.at[k])
        for k, (src, dst) in enumerate(
            (
                (hidden, hid_v),
                (enc_weight, encw_v),
                (local_tiles, lt_v),
                (halo_tiles, ht_v),
                (dec_weight, decw_v),
                (targets, tgt_v),
            )
        )
    ]
    for load in loads:
        load.start()

    def build_onehot(b, carry):
        row = jnp.broadcast_to(send_index[pl.ds(b, 1), :], (BLK, BLK))
        column = jnp.transpose(row)
        for j in range(8):
            hit = column == iota((BLK, BLK), 1) + j * BLK
            onehot[b, :, j * BLK : (j + 1) * BLK] = jnp.where(hit, 1.0, 0.0).astype(BF16)
        return carry

    lax.fori_loop(0, 8, build_onehot, 0)

    loads[0].wait()
    loads[1].wait()

    def encode(c, carry):
        rows = hid_v[pl.ds(c * 2, 2)].reshape(2 * BLK, 512)
        made = jnp.dot(rows, encw_v[...], preferred_element_type=F32).astype(BF16)
        enc[pl.ds(c * 2, 2)] = made.reshape(2, BLK, 512)
        return carry

    lax.fori_loop(0, 4, encode, 0)

    pl.semaphore_wait(barrier, 46)

    def wide_dom(x, z):
        return pltpu.make_async_remote_copy(
            src_ref=out_wide.at[x, pl.ds(z * 16, 16)],
            dst_ref=in_wide.at[mx, pl.ds(mz * 16, 16)],
            send_sem=send_wide.at[x * 8 + z],
            recv_sem=recv_wide.at[md],
            device_id=(mg, x * 8 + z),
            device_id_type=pl.DeviceIdType.MESH,
        )

    def wide_group(q, r):
        return pltpu.make_async_remote_copy(
            src_ref=out_wide.at[4 + q, pl.ds(r * 32, 32)],
            dst_ref=in_wide.at[4 + mq, pl.ds((mg % 4) * 32, 32)],
            send_sem=send_wide.at[32 + q * 4 + r],
            recv_sem=recv_wide.at[32 + mg],
            device_id=(q * 4 + r, md),
            device_id_type=pl.DeviceIdType.MESH,
        )

    def thin_dom(x, z):
        return pltpu.make_async_remote_copy(
            src_ref=out_thin.at[x, pl.ds(z * 16, 16)],
            dst_ref=in_thin.at[mx, pl.ds(mz * 16, 16)],
            send_sem=send_thin.at[x * 8 + z],
            recv_sem=recv_thin.at[md],
            device_id=(mg, x * 8 + z),
            device_id_type=pl.DeviceIdType.MESH,
        )

    def thin_group(q, r):
        return pltpu.make_async_remote_copy(
            src_ref=out_thin.at[4 + q, pl.ds(r * 32, 32)],
            dst_ref=in_thin.at[4 + mq, pl.ds((mg % 4) * 32, 32)],
            send_sem=send_thin.at[32 + q * 4 + r],
            recv_sem=recv_thin.at[32 + mg],
            device_id=(q * 4 + r, md),
            device_id_type=pl.DeviceIdType.MESH,
        )

    def push(x, q, dom_copy, group_copy):
        for k in range(4):
            for z_step in Z_ORDER[2 * k : 2 * k + 2]:
                z = (mz + z_step) % 8

                @pl.when(x * 8 + z != md)
                def _():
                    dom_copy(x, z).start()

            r = (mg + G_ORDER[k]) % 4

            @pl.when(q * 4 + r != mg)
            def _():
                group_copy(q, r).start()

    def gather_send(source, width, out_ref, dom_copy, group_copy):
        def chunk(c, carry):
            off = jnp.where(c == 0, 2, jnp.where(c == 1, 1, jnp.where(c == 2, 3, 0)))
            x = (mx + off) % 4
            q = (mq + off) % 4
            chosen = jnp.concatenate([onehot[x], onehot[4 + q]], axis=0)
            rows = jnp.dot(chosen, source[...].reshape(1024, width), preferred_element_type=F32)
            rows = rows.astype(BF16)
            out_ref[x] = rows[:BLK]
            out_ref[4 + q] = rows[BLK:]
            push(x, q, dom_copy, group_copy)
            return carry

        lax.fori_loop(0, 4, chunk, 0)

    def keep_own(out_ref, in_ref):
        in_ref[mx, pl.ds(pl.multiple_of(mz * 16, 16), 16)] = out_ref[
            mx, pl.ds(pl.multiple_of(mz * 16, 16), 16)
        ]
        own = pl.multiple_of((mg % 4) * 32, 32)
        in_ref[4 + mq, pl.ds(own, 32)] = out_ref[4 + mq, pl.ds(own, 32)]

    def wait_dom(x, in_ref, send, recv):
        def one(z, carry):
            @pl.when(x * 8 + z != md)
            def _():
                part = in_ref.at[x, pl.ds(z * 16, 16)]
                pltpu.make_async_remote_copy(
                    src_ref=part,
                    dst_ref=part,
                    send_sem=send.at[x * 8 + z],
                    recv_sem=recv.at[x * 8 + z],
                    device_id=(mg, x * 8 + z),
                    device_id_type=pl.DeviceIdType.MESH,
                ).wait_recv()

            return carry

        lax.fori_loop(0, 8, one, 0)

    def wait_group(q, in_ref, send, recv):
        def one(r, carry):
            @pl.when(q * 4 + r != mg)
            def _():
                part = in_ref.at[4 + q, pl.ds(r * 32, 32)]
                pltpu.make_async_remote_copy(
                    src_ref=part,
                    dst_ref=part,
                    send_sem=send.at[32 + q * 4 + r],
                    recv_sem=recv.at[32 + q * 4 + r],
                    device_id=(q * 4 + r, md),
                    device_id_type=pl.DeviceIdType.MESH,
                ).wait_recv()

            return carry

        lax.fori_loop(0, 4, one, 0)

    def spread(product, target, live, total):
        for n in range(8):
            weight = jnp.where((target == n) & live, 1.0, 0.0).astype(F32)
            total[n] += product * weight

    def spread_local(source, total):
        def one(t, carry):
            product = jnp.dot(lt_v[t], source[local_src[0, t]], preferred_element_type=F32)
            spread(product, local_dst[0, t], t < local_count[0], total)
            return carry

        lax.fori_loop(0, 12, one, 0)

    def spread_halo(b, source, total):
        tile = jnp.int32(0)
        for t in range(1, 8):
            tile = jnp.where(halo_src[0, t] == b, t, tile)
        product = jnp.dot(ht_v[tile], source[b], preferred_element_type=F32)
        spread(product, halo_dst[0, tile], tile < 8, total)

    def take_halo(in_ref, send, recv, total):
        def chunk(c, carry):
            off = jnp.where(c == 0, 2, jnp.where(c == 1, 3, jnp.where(c == 2, 1, 0)))
            x = (mx + off) % 4
            q = (mq + off) % 4
            wait_dom(x, in_ref, send, recv)
            spread_halo(x, in_ref, total)
            wait_group(q, in_ref, send, recv)
            spread_halo(4 + q, in_ref, total)
            return carry

        lax.fori_loop(0, 4, chunk, 0)

    def drain(copy_dom, copy_group):
        def one_dom(k, carry):
            d = (md + k) % 32
            copy_dom(d // 8, d % 8).wait_send()
            return carry

        def one_group(k, carry):
            g = (mg + k) % 16
            copy_group(g // 4, g % 4).wait_send()
            return carry

        lax.fori_loop(1, 32, one_dom, 0)
        lax.fori_loop(1, 16, one_group, 0)

    gather_send(enc, 512, out_wide, wide_dom, wide_group)
    keep_own(out_wide, in_wide)

    for n in range(8):
        acc[n] = jnp.broadcast_to(enc_bias[...], (BLK, 512))
        hit = iota((BLK, 256), 0) + n * BLK == remask_nodes[...]
        remasked[n] = jnp.dot(
            jnp.where(hit, 1.0, 0.0).astype(BF16),
            jnp.ones((256, BLK), BF16),
            preferred_element_type=F32,
        )
        acc_thin[n] = jnp.broadcast_to(dec_bias[...], (BLK, BLK))
    masked[...] = jnp.zeros((8, BLK), F32)
    for k in range(4):
        column = jnp.transpose(
            jnp.broadcast_to(mask_nodes[:, k * BLK : (k + 1) * BLK], (BLK, BLK))
        )
        for n in range(8):
            hit = jnp.where(column == iota((BLK, BLK), 1) + n * BLK, 1.0, 0.0)
            masked[n : n + 1] += jnp.sum(hit, axis=0, keepdims=True)

    loads[2].wait()
    loads[3].wait()
    loads[4].wait()
    loads[5].wait()
    spread_local(enc, acc)
    take_halo(in_wide, send_wide, recv_wide, acc)

    def decode(n, carry):
        summed = acc[n]
        latent = jnp.where(summed > 0, summed, enc_slope[...] * summed)
        again = jnp.concatenate([remasked[n]] * 4, axis=1) > 0.5
        decoder_in = jnp.where(again, dec_token[...].astype(F32), latent).astype(BF16)
        narrowed[n] = jnp.dot(decoder_in, decw_v[...], preferred_element_type=F32).astype(BF16)
        return carry

    lax.fori_loop(0, 8, decode, 0)

    gather_send(narrowed, BLK, out_thin, thin_dom, thin_group)
    keep_own(out_thin, in_thin)
    spread_local(narrowed, acc_thin)
    take_halo(in_thin, send_thin, recv_thin, acc_thin)

    ones = jnp.ones((8, BLK), BF16)

    def row_sums(values):
        high = values.astype(BF16)
        low = (values - high.astype(F32)).astype(BF16)
        dims = (((1,), (1,)), ((), ()))
        return lax.dot_general(ones, high, dims, preferred_element_type=F32) + lax.dot_general(
            ones, low, dims, preferred_element_type=F32
        )

    for n in range(8):
        made = acc_thin[n].astype(BF16)
        rebuilt[n] = made
        u = made.astype(F32)
        x = tgt_v[n].astype(F32)
        cosine = (
            row_sums(u * x)
            * (1.0 / BLK)
            * lax.rsqrt(row_sums(u * u) * (1.0 / BLK) + 1e-06)
            * lax.rsqrt(row_sums(x * x) * (1.0 / BLK) + 1e-06)
        )
        error = jnp.where(masked[n : n + 1] > 0.5, (1.0 - cosine[:1]) ** 2, 0.0)
        node_error[n : n + 1] = error

    drain(wide_dom, wide_group)
    drain(thin_dom, thin_group)


def per_device(
    hidden,
    enc_weight,
    enc_bias,
    enc_slope,
    dec_token,
    dec_weight,
    dec_bias,
    targets,
    local_tiles,
    local_src,
    local_dst,
    local_count,
    halo_tiles,
    halo_src,
    halo_dst,
    send_rows,
    cross_rows,
    mask_nodes,
    remask_nodes,
):
    send_index = jnp.concatenate([send_rows.reshape(4, BLK), cross_rows.reshape(4, BLK)], axis=0)
    vmem = pl.BlockSpec(memory_space=pltpu.VMEM)
    smem = pl.BlockSpec(memory_space=pltpu.SMEM)
    far = pl.BlockSpec(memory_space=pl.ANY)
    rebuilt, node_error = pl.pallas_call(
        step_kernel,
        out_shape=(
            jax.ShapeDtypeStruct((8, BLK, BLK), BF16),
            jax.ShapeDtypeStruct((8, BLK), F32),
        ),
        in_specs=[
            far,
            far,
            vmem,
            vmem,
            vmem,
            far,
            vmem,
            far,
            far,
            smem,
            smem,
            smem,
            far,
            smem,
            smem,
            vmem,
            vmem,
            vmem,
        ],
        out_specs=(vmem, vmem),
        scratch_shapes=[
            pltpu.VMEM((8, BLK, 512), BF16),
            pltpu.VMEM((512, 512), BF16),
            pltpu.VMEM((512, BLK), BF16),
            pltpu.VMEM((8, BLK, BLK), BF16),
            pltpu.VMEM((12, BLK, BLK), BF16),
            pltpu.VMEM((8, BLK, BLK), BF16),
            pltpu.VMEM((8, BLK, 512), BF16),
            pltpu.VMEM((8, BLK, 1024), BF16),
            pltpu.VMEM((8, BLK, 512), BF16),
            pltpu.VMEM((8, BLK, 512), BF16),
            pltpu.VMEM((8, BLK, 512), F32),
            pltpu.VMEM((8, BLK, BLK), F32),
            pltpu.VMEM((8, BLK), F32),
            pltpu.VMEM((8, BLK, BLK), BF16),
            pltpu.VMEM((8, BLK, BLK), BF16),
            pltpu.VMEM((8, BLK, BLK), BF16),
            pltpu.VMEM((8, BLK, BLK), F32),
            pltpu.SemaphoreType.DMA((6,)),
            pltpu.SemaphoreType.DMA((48,)),
            pltpu.SemaphoreType.DMA((48,)),
            pltpu.SemaphoreType.DMA((48,)),
            pltpu.SemaphoreType.DMA((48,)),
        ],
        compiler_params=pltpu.CompilerParams(
            collective_id=0, has_side_effects=True, vmem_limit_bytes=56 * 1024 * 1024
        ),
        name="step",
    )(
        hidden.reshape(8, BLK, 512),
        enc_weight,
        enc_bias.reshape(1, 512),
        enc_slope.reshape(1, 512),
        dec_token.reshape(1, 512),
        dec_weight,
        dec_bias.reshape(1, BLK),
        targets.reshape(8, BLK, BLK),
        local_tiles,
        local_src,
        local_dst,
        local_count,
        halo_tiles,
        halo_src,
        halo_dst,
        send_index,
        mask_nodes,
        remask_nodes,
    )
    return rebuilt.reshape(1024, BLK), node_error.reshape(1024)


def solution(mesh):
    both = ("group", "dom")
    in_specs = (
        P(both, None),
        P(),
        P(),
        P(),
        P(),
        P(),
        P(),
        P(both, None),
        P(both, None, None),
        P(both, None),
        P(both, None),
        P(both),
        P(both, None, None),
        P(both, None),
        P(both, None),
        P(both, None),
        P(both, None),
        P(both, None),
        P(both, None),
    )
    out_specs = (P(both, None), P(both))
    return jax.shard_map(
        per_device, mesh=mesh, in_specs=in_specs, out_specs=out_specs, check_vma=False
    )
```

time: 153 us -> 51.8 us (0.34)
  Pallas kernels: 0 us -> 45.8 us
  local copies, waits for them, and re-layouts: 44.6 us -> 3.75 us
  starting transfers between devices: 34.6 us -> 0 us
  other arithmetic: 31.3 us -> 0.61 us
  matrix products: 22.9 us -> 0 us
  waiting for transfers between devices: 16.6 us -> 0 us
    pallas_call x0 -> x1, Pallas kernels: none -> 45.8 us  [per_device(): pl.pallas_call(step_kernel, out_shape=(jax.ShapeDtypeStruct((8, BLK, BLK)...]
    all_to_all x4 -> x0, starting transfers between devices: 34.6 us -> none  [the longest x1 11.3 us: per_device(): lax.all_to_all(encoded[send_rows], 'dom', split_axis=0, concat_axis=0, ti...]
    dynamic_slice x32 -> x0, local copies, waits for them, and re-layouts: 23.5 us -> none  [spread(): summed = lax.map(one_block, jnp.arange(blocks, dtype=jnp.int32))]
    dot_general x34 -> x0, matrix products: 22.9 us -> none  [the longest x32 20.7 us: one_block(): return jnp.dot(chosen, picked, preferred_element_type=jnp.float32)]
    convert_element_type x32 -> x0, other arithmetic: 21.8 us -> none  [one_block(): keep = ((tile_owner == target) & column_live).astype(jnp.bfloat16)]
    all_to_all x4 -> x0, waiting for transfers between devices: 16.6 us -> none  [the longest x1 10.9 us: per_device(): lax.all_to_all(encoded[cross_rows], 'group', split_axis=0, concat_axis=0,...]
    gather x8 -> x0, local copies, waits for them, and re-layouts: 14.1 us -> none  [the longest x4 5.05 us: spread(): picked = source_pool[sources].reshape(tile_count * block_rows, width)]
    another operation x4 -> x0, local copies, waits for them, and re-layouts: 3.26 us -> none
  transfers between devices with their start and end apart: 4 -> 0, of which waited for: 2 -> 0; matrix products, arithmetic and copies ran while one was open for 32% -> 0% of each run, Pallas kernels for 0% -> 0%
where the time goes in v1:
time: 51.8 us; the launch traced here: 51.5 us
  Pallas kernels  45.8 us (88%)
  local copies, waits for them, and re-layouts  3.75 us (7%)
  between operations  1.33 us (3%)
  other arithmetic  0.61 us (1%)
    pallas_call x1, Pallas kernels, per_device(): pl.pallas_call(step_kernel, out_shape=(jax.ShapeDtypeStruct((8, BLK, BLK)...  45.8 us
    unnamed x11, local copies, waits for them, and re-layouts  3.01 us

profile of v1, /device:TPU:1, one launch (start us, length us, event | category | flops | bytes accessed | tf_op | source)
XLA Modules:
  0.0 51.5 jit_solution(12086653720629627248)
XLA Ops:
  0.6 0.0 copy-start.1
  1.3 0.0 copy-start.3
  1.3 0.0 copy-start
  1.3 0.7 %copy-done.3 = bf16[512]{0:T(512)(128)(2,1)S(1)} copy-done((bf16[512]{0:T(512)(128)(2,1)S(1)}, bf16[512]{0:T(512)(128)(2,1)}, u32[]{:S(2)}) %copy-start.3) | copy-done | bytes 1048
  2.0 0.6 %reshape.37.dec_token = bf16[1,512]{1,0:T(2,128)(2,1)} reshape(bf16[512]{0:T(512)(128)(2,1)S(1)} %copy-done.3) | data formatting | bytes 2048 | tf_op jit(solution)/shard_map/reshape | solution.py:442
  2.6 0.0 copy-done.1
  2.6 0.1 reshape.41
  2.6 0.0 copy-done
  2.6 0.1 copy.22
  2.7 0.1 reshape.40
  2.8 0.6 %pad_add_fusion.send_index = s32[8,128]{1,0:T(8,128)} fusion(s32[4,128]{1,0:T(4,128)S(1)} %reshape.41, s32[4,128]{1,0:T(4,128)S(1)} %reshape.40), kind=kLoop, calls=%fused_computation | loop fusion | flops 1024 | bytes 8192 | tf_op jit(solution)/shard_map/concatenate | solution.py:378
  3.4 45.8 %step.1 = (bf16[8,128,128]{2,1,0:T(8,128)(2,1)}, f32[8,128]{1,0:T(8,128)}) custom-call(bf16[8,128,512]{2,1,0:T(8,128)(2,1)} %bitcast.7, bf16[512,512]{1,0:T(8,128)(2,1)} %enc_weight.1, f32[1,512]{1,0:T(1,128)} %bitcast.11, f32[1,512]{1,0:T(1,128)} %bitcast.12, bf16[1,512]{1,0:T(2,128)(2,1)} %reshape.37.dec_token, bf16[512,128]{1,0:T(8,128)(2,1)} %dec_weight.1, ...), custom_call_target="tpu_custom_call" | custom-call | tf_op jit(solution)/shard_map/step/pallas_call | solution.py:382
  49.2 0.0 copy-start.2
  49.2 1.7 %copy.26 = bf16[1024,128]{1,0:T(8,128)(2,1)} copy(bf16[1024,128]{1,0:T(8,128)(2,1)} %bitcast.9) | data formatting | bytes 524288
  50.9 0.0 copy-done.2
  50.9 0.6 %copy.27 = f32[1024]{0:T(1024)} copy(f32[1024]{0:T(1024)S(1)} %bitcast.10) | data formatting | bytes 8192
Async XLA Ops:
  0.6 1.9 %copy-start.1 = (s32[16,32]{1,0:T(8,128)S(1)}, s32[16,32]{1,0:T(8,128)}, u32[]{:S(2)}) copy-start(s32[16,32]{1,0:T(8,128)} %param.35) | copy-start | bytes 6148
  1.3 0.7 %copy-start.3 = (bf16[512]{0:T(512)(128)(2,1)S(1)}, bf16[512]{0:T(512)(128)(2,1)}, u32[]{:S(2)}) copy-start(bf16[512]{0:T(512)(128)(2,1)} %param.23) | copy-start | bytes 3076
  1.3 1.3 %copy-start = (s32[32,16]{0,1:T(8,128)S(1)}, s32[32,16]{0,1:T(8,128)}, u32[]{:S(2)}) copy-start(s32[32,16]{0,1:T(8,128)} %param.34) | copy-start | bytes 6148
  49.2 1.7 %copy-start.2 = (f32[8,128]{1,0:T(8,128)S(1)}, f32[8,128]{1,0:T(8,128)}, u32[]{:S(2)}) copy-start(f32[8,128]{1,0:T(8,128)} %get-tuple-element.5) | copy-start | bytes 12292

commit v2 on v1

v2 whole, which is shorter than its diff:
```python
import jax
import jax.numpy as jnp
from jax import lax
from jax.experimental import pallas as pl
from jax.experimental.pallas import tpu as pltpu
from jax.sharding import PartitionSpec as P

BLK = 128
F32 = jnp.float32
BF16 = jnp.bfloat16
I32 = jnp.int32
Z_ORDER = (4, 3, 5, 2, 6, 1, 7, 0)
G_ORDER = (0, 1, 2, 3)


def iota(shape, axis):
    return lax.broadcasted_iota(I32, shape, axis)


def step_kernel(
    hidden,
    enc_weight,
    enc_bias,
    enc_slope,
    dec_token,
    dec_weight,
    dec_bias,
    targets,
    local_tiles,
    local_src,
    local_dst,
    local_count,
    halo_tiles,
    halo_src,
    halo_dst,
    send_rows,
    cross_rows,
    mask_nodes,
    remask_nodes,
    rebuilt,
    node_error,
    hid_v,
    encw_v,
    bias_v,
    slope_v,
    token_v,
    decw_v,
    dbias_v,
    tgt_v,
    lt_v,
    lsrc_s,
    ldst_s,
    ht_v,
    hsrc_s,
    hdst_s,
    send_v,
    cross_v,
    mask_v,
    remask_v,
    square,
    enc,
    onehot,
    out_wide,
    in_wide,
    slots,
    remasked,
    masked,
    norms,
    dots,
    powers,
    narrowed,
    out_thin,
    in_thin,
    slots_thin,
    prev_s,
    final_s,
    tile_s,
    load_sem,
    send_wide,
    recv_wide,
    send_thin,
    recv_thin,
):
    mg = lax.axis_index("group")
    md = lax.axis_index("dom")
    mx = md // 8
    mz = md % 8
    mq = mg // 4

    names = ("send", "cross", "hidden", "encw", "mask", "remask", "lsrc", "ldst")
    names += ("hsrc", "hdst", "bias", "tiles", "tgt", "halo", "slope", "token", "decw", "dbias")
    pairs = (
        (send_rows, send_v),
        (cross_rows, cross_v),
        (hidden, hid_v),
        (enc_weight, encw_v),
        (mask_nodes, mask_v),
        (remask_nodes, remask_v),
        (local_src, lsrc_s),
        (local_dst, ldst_s),
        (halo_src, hsrc_s),
        (halo_dst, hdst_s),
        (enc_bias, bias_v),
        (local_tiles, lt_v),
        (targets, tgt_v),
        (halo_tiles, ht_v),
        (enc_slope, slope_v),
        (dec_token, token_v),
        (dec_weight, decw_v),
        (dec_bias, dbias_v),
    )
    loads = {
        name: pltpu.make_async_copy(src, dst, load_sem.at[k])
        for k, (name, (src, dst)) in enumerate(zip(names, pairs))
    }
    for name in names:
        loads[name].start()

    barrier = pltpu.get_barrier_semaphore()

    def greet_dom(k, carry):
        pl.semaphore_signal(
            barrier, inc=1, device_id=(mg, (md + k) % 32), device_id_type=pl.DeviceIdType.MESH
        )
        return carry

    def greet_group(k, carry):
        pl.semaphore_signal(
            barrier, inc=1, device_id=((mg + k) % 16, md), device_id_type=pl.DeviceIdType.MESH
        )
        return carry

    with jax.named_scope("greet"):
        lax.fori_loop(1, 32, greet_dom, 0)
        lax.fori_loop(1, 16, greet_group, 0)

    def set_rows(row, count, column):
        for j in range(8):
            hit = jnp.broadcast_to(column, (count, BLK)) == iota((count, BLK), 1) + j * BLK
            onehot[row : row + count, j * BLK : (j + 1) * BLK] = jnp.where(hit, 1.0, 0.0).astype(
                BF16
            )

    with jax.named_scope("onehot"):
        loads["send"].wait()
        loads["cross"].wait()
        square[...] = jnp.zeros((BLK, BLK), I32)
        square[0:16, 0:32] = cross_v[...]
        turned = jnp.transpose(square[...])
        for p in range(32):
            set_rows(p * 16, 16, send_v[:, p : p + 1])
        for k in range(16):
            set_rows(512 + k * 32, 32, turned[0:32, k : k + 1])

    with jax.named_scope("load"):
        loads["hidden"].wait()
        loads["encw"].wait()

    def encode(c, carry):
        rows = hid_v[pl.ds(c * 2, 2)].reshape(2 * BLK, 512)
        made = jnp.dot(rows, encw_v[...], preferred_element_type=F32).astype(BF16)
        enc[pl.ds(c * 2, 2)] = made.reshape(2, BLK, 512)
        return carry

    with jax.named_scope("encode"):
        lax.fori_loop(0, 4, encode, 0)

    def dom_copy(out_ref, in_ref, send, recv, d):
        return pltpu.make_async_remote_copy(
            src_ref=out_ref.at[pl.ds(d * 16, 16)],
            dst_ref=in_ref.at[pl.ds(md * 16, 16)],
            send_sem=send,
            recv_sem=recv.at[md],
            device_id=(mg, d),
            device_id_type=pl.DeviceIdType.MESH,
        )

    def group_copy(out_ref, in_ref, send, recv, g):
        return pltpu.make_async_remote_copy(
            src_ref=out_ref.at[pl.ds(512 + g * 32, 32)],
            dst_ref=in_ref.at[pl.ds(512 + mg * 32, 32)],
            send_sem=send,
            recv_sem=recv.at[32 + mg],
            device_id=(g, md),
            device_id_type=pl.DeviceIdType.MESH,
        )

    wide = (out_wide, in_wide, send_wide, recv_wide)
    thin = (out_thin, in_thin, send_thin, recv_thin)

    def push(x, q, ends):
        for k in range(4):
            for z_step in Z_ORDER[2 * k : 2 * k + 2]:
                d = x * 8 + (mz + z_step) % 8

                @pl.when(d != md)
                def _():
                    dom_copy(*ends, d).start()

            g = q * 4 + (mg + G_ORDER[k]) % 4

            @pl.when(g != mg)
            def _():
                group_copy(*ends, g).start()

    def offset(c):
        return jnp.where(c == 0, 2, jnp.where(c == 1, 1, jnp.where(c == 2, 3, 0)))

    def keep_own(out_ref, in_ref):
        own = pl.ds(pl.multiple_of(md * 16, 16), 16)
        in_ref[own] = out_ref[own]
        own = pl.ds(pl.multiple_of(512 + mg * 32, 32), 32)
        in_ref[own] = out_ref[own]

    def wait_dom(x, ends):
        out_ref, in_ref, send, recv = ends

        def one(z, carry):
            d = x * 8 + z

            @pl.when(d != md)
            def _():
                part = in_ref.at[pl.ds(d * 16, 16)]
                pltpu.make_async_remote_copy(
                    src_ref=part,
                    dst_ref=part,
                    send_sem=send,
                    recv_sem=recv.at[d],
                    device_id=(mg, d),
                    device_id_type=pl.DeviceIdType.MESH,
                ).wait_recv()

            return carry

        lax.fori_loop(0, 8, one, 0)

    def wait_group(q, ends):
        out_ref, in_ref, send, recv = ends

        def one(r, carry):
            g = q * 4 + r

            @pl.when(g != mg)
            def _():
                part = in_ref.at[pl.ds(512 + g * 32, 32)]
                pltpu.make_async_remote_copy(
                    src_ref=part,
                    dst_ref=part,
                    send_sem=send,
                    recv_sem=recv.at[32 + g],
                    device_id=(g, md),
                    device_id_type=pl.DeviceIdType.MESH,
                ).wait_recv()

            return carry

        lax.fori_loop(0, 4, one, 0)

    def drain(ends):
        out_ref, in_ref, send, recv = ends
        part = out_ref.at[pl.ds(0, 976)]
        pltpu.make_async_remote_copy(
            src_ref=part,
            dst_ref=part,
            send_sem=send,
            recv_sem=recv.at[0],
            device_id=(mg, md),
            device_id_type=pl.DeviceIdType.MESH,
        ).wait_send()

    def gather_all(c, carry):
        at = pl.ds(pl.multiple_of(c * 256, 256), 256)
        rows = jnp.dot(onehot[at], enc[...].reshape(1024, 512), preferred_element_type=F32)
        out_wide[at] = rows.astype(BF16)
        return carry

    with jax.named_scope("gather_wide"):
        lax.fori_loop(0, 4, gather_all, 0)

    with jax.named_scope("chain"):
        for name in ("lsrc", "ldst", "hsrc", "hdst"):
            loads[name].wait()
        goals = [jnp.where(t < local_count[0], ldst_s[0, t], 8) for t in range(12)]
        for c, off in enumerate((2, 3, 1, 0)):
            for half, b in enumerate(((mx + off) % 4, 4 + (mq + off) % 4)):
                tile = jnp.int32(0)
                for t in range(1, 8):
                    tile = jnp.where(hsrc_s[0, t] == b, t, tile)
                tile_s[2 * c + half] = tile
                goals.append(hdst_s[0, tile])
        for j in range(20):
            prev = jnp.minimum(goals[j], 7)
            for i in range(j):
                prev = jnp.where(goals[i] == goals[j], 8 + i, prev)
            prev_s[j] = prev
        for n in range(8):
            last = jnp.int32(n)
            for i in range(20):
                last = jnp.where(goals[i] == n, 8 + i, last)
            final_s[n] = last

    with jax.named_scope("masks"):
        loads["mask"].wait()
        loads["remask"].wait()
        for n in range(8):
            hit = iota((BLK, 256), 0) + n * BLK == remask_v[...]
            remasked[n] = jnp.dot(
                jnp.where(hit, 1.0, 0.0).astype(BF16),
                jnp.ones((256, BLK), BF16),
                preferred_element_type=F32,
            )
        masked[...] = jnp.zeros((8, BLK), F32)
        for k in range(4):
            column = jnp.transpose(
                jnp.broadcast_to(mask_v[:, k * BLK : (k + 1) * BLK], (BLK, BLK))
            )
            for n in range(8):
                hit = jnp.where(column == iota((BLK, BLK), 1) + n * BLK, 1.0, 0.0)
                masked[n : n + 1] += jnp.sum(hit, axis=0, keepdims=True)

    with jax.named_scope("barrier"):
        pl.semaphore_wait(barrier, 46)

    def push_chunk(c, carry):
        off = offset(c)
        push((mx + off) % 4, (mq + off) % 4, wide)
        return carry

    with jax.named_scope("push"):
        lax.fori_loop(0, 4, push_chunk, 0)
        keep_own(out_wide, in_wide)

    def row_sums(values):
        column = jnp.sum(values, axis=1, keepdims=True)
        on = iota((BLK, BLK), 0) == iota((BLK, BLK), 1)
        return jnp.sum(jnp.where(on, column, 0.0), axis=0, keepdims=True)

    with jax.named_scope("norms"):
        for name in ("bias", "tiles", "tgt", "halo", "slope", "token", "decw", "dbias"):
            loads[name].wait()
        for n in range(8):
            slots[n] = jnp.broadcast_to(bias_v[...], (BLK, 512))
            slots_thin[n] = jnp.broadcast_to(dbias_v[...], (BLK, BLK))
            x = tgt_v[n].astype(F32)
            norms[n : n + 1] = row_sums(x * x)

    def spread_local(source, total):
        def one(t, carry):
            product = jnp.dot(lt_v[t], source[lsrc_s[0, t]], preferred_element_type=F32)
            total[8 + t] = total[prev_s[t]] + product
            return carry

        lax.fori_loop(0, 12, one, 0)

    def take_halo(ends, total):
        in_ref = ends[1]

        def spread(j, b):
            rows = in_ref[pl.ds(pl.multiple_of(b * BLK, BLK), BLK)]
            product = jnp.dot(ht_v[tile_s[j]], rows, preferred_element_type=F32)
            total[20 + j] = total[prev_s[12 + j]] + product

        def chunk(c, carry):
            off = jnp.where(c == 0, 2, jnp.where(c == 1, 3, jnp.where(c == 2, 1, 0)))
            x = (mx + off) % 4
            q = (mq + off) % 4
            with jax.named_scope("wait_dom"):
                wait_dom(x, ends)
            spread(2 * c, x)
            with jax.named_scope("wait_group"):
                wait_group(q, ends)
            spread(2 * c + 1, 4 + q)
            return carry

        lax.fori_loop(0, 4, chunk, 0)

    with jax.named_scope("local_wide"):
        spread_local(enc, slots)
    with jax.named_scope("halo_wide"):
        take_halo(wide, slots)

    token = token_v[...].astype(F32).reshape(1, 512)

    def decode(n, carry):
        summed = slots[final_s[n]]
        latent = jnp.where(summed > 0, summed, slope_v[...] * summed)
        again = jnp.concatenate([remasked[n]] * 4, axis=1) > 0.5
        decoder_in = jnp.where(again, token, latent).astype(BF16)
        narrowed[n] = jnp.dot(decoder_in, decw_v[...], preferred_element_type=F32).astype(BF16)
        return carry

    with jax.named_scope("decode"):
        lax.fori_loop(0, 8, decode, 0)

    def gather_thin(c, carry):
        off = offset(c)
        x = (mx + off) % 4
        q = (mq + off) % 4
        upper = pl.ds(pl.multiple_of(x * BLK, BLK), BLK)
        lower = pl.ds(pl.multiple_of((4 + q) * BLK, BLK), BLK)
        chosen = jnp.concatenate([onehot[upper], onehot[lower]], axis=0)
        rows = jnp.dot(chosen, narrowed[...].reshape(1024, BLK), preferred_element_type=F32)
        rows = rows.astype(BF16)
        out_thin[upper] = rows[:BLK]
        out_thin[lower] = rows[BLK:]
        push(x, q, thin)
        return carry

    with jax.named_scope("gather_thin"):
        lax.fori_loop(0, 4, gather_thin, 0)
        keep_own(out_thin, in_thin)
    with jax.named_scope("local_thin"):
        spread_local(narrowed, slots_thin)
        drain(wide)
    with jax.named_scope("halo_thin"):
        take_halo(thin, slots_thin)

    with jax.named_scope("errors"):
        for n in range(8):
            made = slots_thin[final_s[n]].astype(BF16)
            rebuilt[n] = made
            u = made.astype(F32)
            x = tgt_v[n].astype(F32)
            dots[n : n + 1] = row_sums(u * x)
            powers[n : n + 1] = row_sums(u * u)
        cosine = (
            dots[...]
            * (1.0 / BLK)
            * lax.rsqrt(powers[...] * (1.0 / BLK) + 1e-06)
            * lax.rsqrt(norms[...] * (1.0 / BLK) + 1e-06)
        )
        node_error[...] = jnp.where(masked[...] > 0.5, (1.0 - cosine) ** 2, 0.0)

    with jax.named_scope("drain"):
        drain(thin)


def per_device(
    hidden,
    enc_weight,
    enc_bias,
    enc_slope,
    dec_token,
    dec_weight,
    dec_bias,
    targets,
    local_tiles,
    local_src,
    local_dst,
    local_count,
    halo_tiles,
    halo_src,
    halo_dst,
    send_rows,
    cross_rows,
    mask_nodes,
    remask_nodes,
):
    vmem = pl.BlockSpec(memory_space=pltpu.VMEM)
    smem = pl.BlockSpec(memory_space=pltpu.SMEM)
    far = pl.BlockSpec(memory_space=pl.ANY)
    rebuilt, node_error = pl.pallas_call(
        step_kernel,
        out_shape=(
            pltpu.VMEM((8, BLK, BLK), BF16),
            pltpu.VMEM((8, BLK), F32),
        ),
        in_specs=[far] * 11 + [smem] + [far] * 7,
        out_specs=(vmem, vmem),
        scratch_shapes=[
            pltpu.VMEM((8, BLK, 512), BF16),
            pltpu.VMEM((512, 512), BF16),
            pltpu.VMEM((1, 512), F32),
            pltpu.VMEM((1, 512), F32),
            pltpu.VMEM((512,), BF16),
            pltpu.VMEM((512, BLK), BF16),
            pltpu.VMEM((1, BLK), F32),
            pltpu.VMEM((8, BLK, BLK), BF16),
            pltpu.VMEM((12, BLK, BLK), BF16),
            pltpu.SMEM((1, 12), I32),
            pltpu.SMEM((1, 12), I32),
            pltpu.VMEM((8, BLK, BLK), BF16),
            pltpu.SMEM((1, 8), I32),
            pltpu.SMEM((1, 8), I32),
            pltpu.VMEM((16, 32), I32),
            pltpu.VMEM((16, 32), I32),
            pltpu.VMEM((1, 512), I32),
            pltpu.VMEM((1, 256), I32),
            pltpu.VMEM((BLK, BLK), I32),
            pltpu.VMEM((8, BLK, 512), BF16),
            pltpu.VMEM((1024, 1024), BF16),
            pltpu.VMEM((1024, 512), BF16),
            pltpu.VMEM((1024, 512), BF16),
            pltpu.VMEM((28, BLK, 512), F32),
            pltpu.VMEM((8, BLK, BLK), F32),
            pltpu.VMEM((8, BLK), F32),
            pltpu.VMEM((8, BLK), F32),
            pltpu.VMEM((8, BLK), F32),
            pltpu.VMEM((8, BLK), F32),
            pltpu.VMEM((8, BLK, BLK), BF16),
            pltpu.VMEM((1024, BLK), BF16),
            pltpu.VMEM((1024, BLK), BF16),
            pltpu.VMEM((28, BLK, BLK), F32),
            pltpu.SMEM((20,), I32),
            pltpu.SMEM((8,), I32),
            pltpu.SMEM((8,), I32),
            pltpu.SemaphoreType.DMA((18,)),
            pltpu.SemaphoreType.DMA,
            pltpu.SemaphoreType.DMA((48,)),
            pltpu.SemaphoreType.DMA,
            pltpu.SemaphoreType.DMA((48,)),
        ],
        compiler_params=pltpu.CompilerParams(
            collective_id=0, has_side_effects=True, vmem_limit_bytes=56 * 1024 * 1024
        ),
        name="step",
    )(
        hidden.reshape(8, BLK, 512),
        enc_weight,
        enc_bias.reshape(1, 512),
        enc_slope.reshape(1, 512),
        dec_token,
        dec_weight,
        dec_bias.reshape(1, BLK),
        targets.reshape(8, BLK, BLK),
        local_tiles,
        local_src,
        local_dst,
        local_count,
        halo_tiles,
        halo_src,
        halo_dst,
        send_rows.T,
        cross_rows,
        mask_nodes,
        remask_nodes,
    )
    return rebuilt.reshape(1024, BLK), node_error.reshape(1024)


def solution(mesh):
    both = ("group", "dom")
    in_specs = (
        P(both, None),
        P(),
        P(),
        P(),
        P(),
        P(),
        P(),
        P(both, None),
        P(both, None, None),
        P(both, None),
        P(both, None),
        P(both),
        P(both, None, None),
        P(both, None),
        P(both, None),
        P(both, None),
        P(both, None),
        P(both, None),
        P(both, None),
    )
    out_specs = (P(both, None), P(both))
    return jax.shard_map(
        per_device, mesh=mesh, in_specs=in_specs, out_specs=out_specs, check_vma=False
    )
```

time: 51.8 us -> 43.7 us (0.84)
  Pallas kernels: 45.8 us -> 40.9 us
  local copies, waits for them, and re-layouts: 3.75 us -> 1.3 us
  other arithmetic: 0.61 us -> 0 us
    pallas_call x1, Pallas kernels: 45.8 us -> 40.9 us  [per_device(): pl.pallas_call(step_kernel, out_shape=(pltpu.VMEM((8, BLK, BLK), BF16), p...]
    unnamed x11 -> x2, local copies, waits for them, and re-layouts: 3.01 us -> 1.3 us
    reshape x3 -> x0, local copies, waits for them, and re-layouts: 0.74 us -> none  [the longest x1 0.58 us: per_device(): dec_token.reshape(1, 512)]
    concatenate x1 -> x0, other arithmetic: 0.61 us -> none  [per_device(): jnp.concatenate([send_rows.reshape(4, BLK), cross_rows.reshape(4, BLK)],...]
where the time goes in v2:
time: 43.7 us; the launch traced here: 43.5 us
  Pallas kernels  40.9 us (94%)
  local copies, waits for them, and re-layouts  1.3 us (3%)
  between operations  1.29 us (3%)
    pallas_call x1, Pallas kernels, per_device(): pl.pallas_call(step_kernel, out_shape=(pltpu.VMEM((8, BLK, BLK), BF16), p...  40.9 us
    unnamed x2, local copies, waits for them, and re-layouts  1.3 us

profile of v2, /device:TPU:1, one launch (start us, length us, event | category | flops | bytes accessed | tf_op | source)
XLA Modules:
  0.0 43.5 jit_solution(2678249689999000738)
XLA Ops:
  1.3 40.9 %step.1 = (bf16[8,128,128]{2,1,0:T(8,128)(2,1)S(1)}, f32[8,128]{1,0:T(8,128)S(1)}) custom-call(bf16[8,128,512]{2,1,0:T(8,128)(2,1)} %bitcast.10, bf16[512,512]{1,0:T(8,128)(2,1)} %enc_weight.1, f32[1,512]{1,0:T(1,128)} %bitcast.13, f32[1,512]{1,0:T(1,128)} %bitcast.14, bf16[512]{0:T(512)(128)(2,1)} %dec_token.1, bf16[512,128]{1,0:T(8,128)(2,1)} %dec_weight.1, ...), custom_call_target="tpu_custom_call" | custom-call | tf_op jit(solution)/shard_map/step/pallas_call | solution.py:462
  42.2 0.7 %copy.23 = bf16[1024,128]{1,0:T(8,128)(2,1)} copy(bf16[1024,128]{1,0:T(8,128)(2,1)S(1)} %bitcast.8) | data formatting | bytes 524288
  42.9 0.6 %copy.24 = f32[1024]{0:T(1024)} copy(f32[1024]{0:T(1024)S(1)} %bitcast.9) | data formatting | bytes 8192

commit v3 on v2

--- a/solution.py
+++ b/solution.py
@@ -9,8 +9,10 @@
 F32 = jnp.float32
 BF16 = jnp.bfloat16
 I32 = jnp.int32
-Z_ORDER = (4, 3, 5, 2, 6, 1, 7, 0)
-G_ORDER = (0, 1, 2, 3)
+FAR_X = (2, 1, 3, 0)
+FAR_8 = (4, 3, 5, 2, 6, 1, 7, 0)
+FAR_DOM = tuple((x, z) for x in FAR_X for z in FAR_8 if x or z)
+FAR_GROUP = tuple((y, c) for y in FAR_8 for c in (1, 0) if y or c)
 
 
 def iota(shape, axis):
@@ -50,6 +52,7 @@
     lt_v,
     lsrc_s,
     ldst_s,
+    lcnt_s,
     ht_v,
     hsrc_s,
     hdst_s,
@@ -72,6 +75,7 @@
     out_thin,
     in_thin,
     slots_thin,
+    products,
     prev_s,
     final_s,
     tile_s,
@@ -85,9 +89,26 @@
     md = lax.axis_index("dom")
     mx = md // 8
     mz = md % 8
+    my = mg // 2
+    mc = mg % 2
     mq = mg // 4
 
-    names = ("send", "cross", "hidden", "encw", "mask", "remask", "lsrc", "ldst")
+    def turn(at, by, size):
+        return jnp.where(at + by >= size, at + by - size, at + by)
+
+    xs = [turn(mx, k, 4) for k in range(4)]
+    zs = [turn(mz, k, 8) for k in range(8)]
+    ys = [turn(my, k, 8) for k in range(8)]
+    qs = [turn(mq, k, 4) for k in range(4)]
+    cs = [mc, 1 - mc]
+
+    def dom_at(x, z):
+        return xs[x] * 8 + zs[z]
+
+    def group_at(y, c):
+        return ys[y] * 2 + cs[c]
+
+    names = ("send", "cross", "hidden", "encw", "mask", "remask", "lsrc", "ldst", "lcnt")
     names += ("hsrc", "hdst", "bias", "tiles", "tgt", "halo", "slope", "token", "decw", "dbias")
     pairs = (
         (send_rows, send_v),
@@ -98,6 +119,7 @@
         (remask_nodes, remask_v),
         (local_src, lsrc_s),
         (local_dst, ldst_s),
+        (local_count, lcnt_s),
         (halo_src, hsrc_s),
         (halo_dst, hdst_s),
         (enc_bias, bias_v),
@@ -118,21 +140,21 @@
 
     barrier = pltpu.get_barrier_semaphore()
 
-    def greet_dom(k, carry):
-        pl.semaphore_signal(
-            barrier, inc=1, device_id=(mg, (md + k) % 32), device_id_type=pl.DeviceIdType.MESH
-        )
-        return carry
-
-    def greet_group(k, carry):
-        pl.semaphore_signal(
-            barrier, inc=1, device_id=((mg + k) % 16, md), device_id_type=pl.DeviceIdType.MESH
-        )
-        return carry
-
     with jax.named_scope("greet"):
-        lax.fori_loop(1, 32, greet_dom, 0)
-        lax.fori_loop(1, 16, greet_group, 0)
+        for x, z in FAR_DOM:
+            pl.semaphore_signal(
+                barrier,
+                inc=1,
+                device_id=(mg, dom_at(x, z)),
+                device_id_type=pl.DeviceIdType.MESH,
+            )
+        for y, c in FAR_GROUP:
+            pl.semaphore_signal(
+                barrier,
+                inc=1,
+                device_id=(group_at(y, c), md),
+                device_id_type=pl.DeviceIdType.MESH,
+            )
 
     def set_rows(row, count, column):
         for j in range(8):
@@ -154,23 +176,23 @@
 
     with jax.named_scope("load"):
         loads["hidden"].wait()
+
+    def encode(c, carry):
+        rows = hid_v[pl.ds(c * 4, 4)].reshape(4 * BLK, 512)
+        made = jnp.dot(rows, encw_v[...], preferred_element_type=F32).astype(BF16)
+        enc[pl.ds(c * 4, 4)] = made.reshape(4, BLK, 512)
+        return carry
+
+    with jax.named_scope("encode"):
         loads["encw"].wait()
-
-    def encode(c, carry):
-        rows = hid_v[pl.ds(c * 2, 2)].reshape(2 * BLK, 512)
-        made = jnp.dot(rows, encw_v[...], preferred_element_type=F32).astype(BF16)
-        enc[pl.ds(c * 2, 2)] = made.reshape(2, BLK, 512)
-        return carry
-
-    with jax.named_scope("encode"):
-        lax.fori_loop(0, 4, encode, 0)
+        lax.fori_loop(0, 2, encode, 0)
 
     def dom_copy(out_ref, in_ref, send, recv, d):
         return pltpu.make_async_remote_copy(
             src_ref=out_ref.at[pl.ds(d * 16, 16)],
             dst_ref=in_ref.at[pl.ds(md * 16, 16)],
             send_sem=send,
-            recv_sem=recv.at[md],
+            recv_sem=recv,
             device_id=(mg, d),
             device_id_type=pl.DeviceIdType.MESH,
         )
@@ -180,31 +202,14 @@
             src_ref=out_ref.at[pl.ds(512 + g * 32, 32)],
             dst_ref=in_ref.at[pl.ds(512 + mg * 32, 32)],
             send_sem=send,
-            recv_sem=recv.at[32 + mg],
+            recv_sem=recv,
             device_id=(g, md),
             device_id_type=pl.DeviceIdType.MESH,
         )
 
-    wide = (out_wide, in_wide, send_wide, recv_wide)
+    wide_dom = (out_wide, in_wide, send_wide, recv_wide.at[mx])
+    wide_group = (out_wide, in_wide, send_wide, recv_wide.at[4 + mq])
     thin = (out_thin, in_thin, send_thin, recv_thin)
-
-    def push(x, q, ends):
-        for k in range(4):
-            for z_step in Z_ORDER[2 * k : 2 * k + 2]:
-                d = x * 8 + (mz + z_step) % 8
-
-                @pl.when(d != md)
-                def _():
-                    dom_copy(*ends, d).start()
-
-            g = q * 4 + (mg + G_ORDER[k]) % 4
-
-            @pl.when(g != mg)
-            def _():
-                group_copy(*ends, g).start()
-
-    def offset(c):
-        return jnp.where(c == 0, 2, jnp.where(c == 1, 1, jnp.where(c == 2, 3, 0)))
 
     def keep_own(out_ref, in_ref):
         own = pl.ds(pl.multiple_of(md * 16, 16), 16)
@@ -212,77 +217,63 @@
         own = pl.ds(pl.multiple_of(512 + mg * 32, 32), 32)
         in_ref[own] = out_ref[own]
 
-    def wait_dom(x, ends):
-        out_ref, in_ref, send, recv = ends
-
-        def one(z, carry):
-            d = x * 8 + z
-
-            @pl.when(d != md)
-            def _():
-                part = in_ref.at[pl.ds(d * 16, 16)]
-                pltpu.make_async_remote_copy(
-                    src_ref=part,
-                    dst_ref=part,
-                    send_sem=send,
-                    recv_sem=recv.at[d],
-                    device_id=(mg, d),
-                    device_id_type=pl.DeviceIdType.MESH,
-                ).wait_recv()
-
-            return carry
-
-        lax.fori_loop(0, 8, one, 0)
-
-    def wait_group(q, ends):
-        out_ref, in_ref, send, recv = ends
-
-        def one(r, carry):
-            g = q * 4 + r
-
-            @pl.when(g != mg)
-            def _():
-                part = in_ref.at[pl.ds(512 + g * 32, 32)]
-                pltpu.make_async_remote_copy(
-                    src_ref=part,
-                    dst_ref=part,
-                    send_sem=send,
-                    recv_sem=recv.at[32 + g],
-                    device_id=(g, md),
-                    device_id_type=pl.DeviceIdType.MESH,
-                ).wait_recv()
-
-            return carry
-
-        lax.fori_loop(0, 4, one, 0)
-
-    def drain(ends):
-        out_ref, in_ref, send, recv = ends
+    def await_rows(in_ref, count, send, recv):
+        part = in_ref.at[pl.ds(0, count)]
+        pltpu.make_async_remote_copy(
+            src_ref=part,
+            dst_ref=part,
+            send_sem=send,
+            recv_sem=recv,
+            device_id=(mg, md),
+            device_id_type=pl.DeviceIdType.MESH,
+        ).wait_recv()
+
+    def await_block(b, own, fewer):
+        @pl.when(b == own)
+        def _():
+            await_rows(in_wide, fewer, send_wide, recv_wide.at[b])
+
+        @pl.when(b != own)
+        def _():
+            await_rows(in_wide, BLK, send_wide, recv_wide.at[b])
+
+    def drain(out_ref, send, recv):
         part = out_ref.at[pl.ds(0, 976)]
         pltpu.make_async_remote_copy(
             src_ref=part,
             dst_ref=part,
             send_sem=send,
-            recv_sem=recv.at[0],
+            recv_sem=recv,
             device_id=(mg, md),
             device_id_type=pl.DeviceIdType.MESH,
         ).wait_send()
 
     def gather_all(c, carry):
-        at = pl.ds(pl.multiple_of(c * 256, 256), 256)
+        at = pl.ds(pl.multiple_of(c * 512, 512), 512)
         rows = jnp.dot(onehot[at], enc[...].reshape(1024, 512), preferred_element_type=F32)
         out_wide[at] = rows.astype(BF16)
         return carry
 
     with jax.named_scope("gather_wide"):
-        lax.fori_loop(0, 4, gather_all, 0)
+        lax.fori_loop(0, 2, gather_all, 0)
+
+    with jax.named_scope("barrier"):
+        pl.semaphore_wait(barrier, 46)
+
+    with jax.named_scope("push"):
+        for k in range(16):
+            if k < 15:
+                group_copy(*wide_group, group_at(*FAR_GROUP[k])).start()
+            for x, z in FAR_DOM[2 * k : 2 * k + 2]:
+                dom_copy(*wide_dom, dom_at(x, z)).start()
+        keep_own(out_wide, in_wide)
 
     with jax.named_scope("chain"):
-        for name in ("lsrc", "ldst", "hsrc", "hdst"):
+        for name in ("lsrc", "ldst", "lcnt", "hsrc", "hdst"):
             loads[name].wait()
-        goals = [jnp.where(t < local_count[0], ldst_s[0, t], 8) for t in range(12)]
+        goals = [jnp.where(t < lcnt_s[0, 0], ldst_s[0, t], 8) for t in range(12)]
         for c, off in enumerate((2, 3, 1, 0)):
-            for half, b in enumerate(((mx + off) % 4, 4 + (mq + off) % 4)):
+            for half, b in enumerate((xs[off], 4 + qs[off])):
                 tile = jnp.int32(0)
                 for t in range(1, 8):
                     tile = jnp.where(hsrc_s[0, t] == b, t, tile)
@@ -318,18 +309,6 @@
                 hit = jnp.where(column == iota((BLK, BLK), 1) + n * BLK, 1.0, 0.0)
                 masked[n : n + 1] += jnp.sum(hit, axis=0, keepdims=True)
 
-    with jax.named_scope("barrier"):
-        pl.semaphore_wait(barrier, 46)
-
-    def push_chunk(c, carry):
-        off = offset(c)
-        push((mx + off) % 4, (mq + off) % 4, wide)
-        return carry
-
-    with jax.named_scope("push"):
-        lax.fori_loop(0, 4, push_chunk, 0)
-        keep_own(out_wide, in_wide)
-
     def row_sums(values):
         column = jnp.sum(values, axis=1, keepdims=True)
         on = iota((BLK, BLK), 0) == iota((BLK, BLK), 1)
@@ -352,68 +331,69 @@
 
         lax.fori_loop(0, 12, one, 0)
 
-    def take_halo(ends, total):
-        in_ref = ends[1]
-
-        def spread(j, b):
-            rows = in_ref[pl.ds(pl.multiple_of(b * BLK, BLK), BLK)]
+    def halo_wide(c, carry):
+        off = jnp.where(c == 0, 2, jnp.where(c == 1, 3, jnp.where(c == 2, 1, 0)))
+        x = (mx + off) % 4
+        q = 4 + (mq + off) % 4
+        for j, b, own, fewer in ((2 * c, x, mx, 112), (2 * c + 1, q, 4 + mq, 96)):
+            with jax.named_scope("await"):
+                await_block(b, own, fewer)
+            rows = in_wide[pl.ds(pl.multiple_of(b * BLK, BLK), BLK)]
             product = jnp.dot(ht_v[tile_s[j]], rows, preferred_element_type=F32)
-            total[20 + j] = total[prev_s[12 + j]] + product
-
-        def chunk(c, carry):
-            off = jnp.where(c == 0, 2, jnp.where(c == 1, 3, jnp.where(c == 2, 1, 0)))
-            x = (mx + off) % 4
-            q = (mq + off) % 4
-            with jax.named_scope("wait_dom"):
-                wait_dom(x, ends)
-            spread(2 * c, x)
-            with jax.named_scope("wait_group"):
-                wait_group(q, ends)
-            spread(2 * c + 1, 4 + q)
-            return carry
-
-        lax.fori_loop(0, 4, chunk, 0)
+            slots[20 + j] = slots[prev_s[12 + j]] + product
+        return carry
 
     with jax.named_scope("local_wide"):
         spread_local(enc, slots)
     with jax.named_scope("halo_wide"):
-        take_halo(wide, slots)
+        lax.fori_loop(0, 4, halo_wide, 0)
 
     token = token_v[...].astype(F32).reshape(1, 512)
 
-    def decode(n, carry):
-        summed = slots[final_s[n]]
-        latent = jnp.where(summed > 0, summed, slope_v[...] * summed)
-        again = jnp.concatenate([remasked[n]] * 4, axis=1) > 0.5
-        decoder_in = jnp.where(again, token, latent).astype(BF16)
-        narrowed[n] = jnp.dot(decoder_in, decw_v[...], preferred_element_type=F32).astype(BF16)
-        return carry
-
     with jax.named_scope("decode"):
-        lax.fori_loop(0, 8, decode, 0)
-
-    def gather_thin(c, carry):
-        off = offset(c)
-        x = (mx + off) % 4
-        q = (mq + off) % 4
-        upper = pl.ds(pl.multiple_of(x * BLK, BLK), BLK)
-        lower = pl.ds(pl.multiple_of((4 + q) * BLK, BLK), BLK)
-        chosen = jnp.concatenate([onehot[upper], onehot[lower]], axis=0)
-        rows = jnp.dot(chosen, narrowed[...].reshape(1024, BLK), preferred_element_type=F32)
-        rows = rows.astype(BF16)
-        out_thin[upper] = rows[:BLK]
-        out_thin[lower] = rows[BLK:]
-        push(x, q, thin)
-        return carry
+        for n in range(8):
+            summed = slots[final_s[n]]
+            latent = jnp.where(summed > 0, summed, slope_v[...] * summed)
+            again = jnp.concatenate([remasked[n]] * 4, axis=1) > 0.5
+            decoder_in = jnp.where(again, token, latent).astype(BF16)
+            narrowed[n] = jnp.dot(decoder_in, decw_v[...], preferred_element_type=F32).astype(BF16)
 
     with jax.named_scope("gather_thin"):
-        lax.fori_loop(0, 4, gather_thin, 0)
+        for x in FAR_X:
+            q = qs[x]
+            upper = pl.ds(pl.multiple_of(xs[x] * BLK, BLK), BLK)
+            lower = pl.ds(pl.multiple_of((4 + q) * BLK, BLK), BLK)
+            chosen = jnp.concatenate([onehot[upper], onehot[lower]], axis=0)
+            rows = jnp.dot(chosen, narrowed[...].reshape(1024, BLK), preferred_element_type=F32)
+            rows = rows.astype(BF16)
+            out_thin[upper] = rows[:BLK]
+            out_thin[lower] = rows[BLK:]
+            for k in range(4):
+                for z in FAR_8[2 * k : 2 * k + 2]:
+                    if x or z:
+                        dom_copy(*thin, dom_at(x, z)).start()
+                g = q * 4 + k
+                if x:
+                    group_copy(*thin, g).start()
+                else:
+
+                    @pl.when(g != mg)
+                    def _(g=g):
+                        group_copy(*thin, g).start()
+
         keep_own(out_thin, in_thin)
     with jax.named_scope("local_thin"):
         spread_local(narrowed, slots_thin)
-        drain(wide)
+        drain(out_wide, send_wide, recv_wide.at[0])
+    with jax.named_scope("await_thin"):
+        await_rows(in_thin, 976, send_thin, recv_thin)
     with jax.named_scope("halo_thin"):
-        take_halo(thin, slots_thin)
+        for c, off in enumerate((2, 3, 1, 0)):
+            for j, b in ((2 * c, xs[off]), (2 * c + 1, 4 + qs[off])):
+                rows = in_thin[pl.ds(pl.multiple_of(b * BLK, BLK), BLK)]
+                products[j] = jnp.dot(ht_v[tile_s[j]], rows, preferred_element_type=F32)
+        for j in range(8):
+            slots_thin[20 + j] = slots_thin[prev_s[12 + j]] + products[j]
 
     with jax.named_scope("errors"):
         for n in range(8):
@@ -432,7 +412,18 @@
         node_error[...] = jnp.where(masked[...] > 0.5, (1.0 - cosine) ** 2, 0.0)
 
     with jax.named_scope("drain"):
-        drain(thin)
+        drain(out_thin, send_thin, recv_thin)
+
+
+def finish_kernel(rebuilt, node_error, rebuilt_out, node_error_out, sem):
+    copies = (
+        pltpu.make_async_copy(rebuilt, rebuilt_out, sem.at[0]),
+        pltpu.make_async_copy(node_error, node_error_out, sem.at[1]),
+    )
+    for copy in copies:
+        copy.start()
+    for copy in copies:
+        copy.wait()
 
 
 def per_device(
@@ -457,7 +448,6 @@
     remask_nodes,
 ):
     vmem = pl.BlockSpec(memory_space=pltpu.VMEM)
-    smem = pl.BlockSpec(memory_space=pltpu.SMEM)
     far = pl.BlockSpec(memory_space=pl.ANY)
     rebuilt, node_error = pl.pallas_call(
         step_kernel,
@@ -465,7 +455,7 @@
             pltpu.VMEM((8, BLK, BLK), BF16),
             pltpu.VMEM((8, BLK), F32),
         ),
-        in_specs=[far] * 11 + [smem] + [far] * 7,
+        in_specs=[far] * 19,
         out_specs=(vmem, vmem),
         scratch_shapes=[
             pltpu.VMEM((8, BLK, 512), BF16),
@@ -479,6 +469,7 @@
             pltpu.VMEM((12, BLK, BLK), BF16),
             pltpu.SMEM((1, 12), I32),
             pltpu.SMEM((1, 12), I32),
+            pltpu.SMEM((1, 1), I32),
             pltpu.VMEM((8, BLK, BLK), BF16),
             pltpu.SMEM((1, 8), I32),
             pltpu.SMEM((1, 8), I32),
@@ -501,14 +492,15 @@
             pltpu.VMEM((1024, BLK), BF16),
             pltpu.VMEM((1024, BLK), BF16),
             pltpu.VMEM((28, BLK, BLK), F32),
+            pltpu.VMEM((8, BLK, BLK), F32),
             pltpu.SMEM((20,), I32),
             pltpu.SMEM((8,), I32),
             pltpu.SMEM((8,), I32),
-            pltpu.SemaphoreType.DMA((18,)),
+            pltpu.SemaphoreType.DMA((19,)),
             pltpu.SemaphoreType.DMA,
-            pltpu.SemaphoreType.DMA((48,)),
+            pltpu.SemaphoreType.DMA((8,)),
             pltpu.SemaphoreType.DMA,
-            pltpu.SemaphoreType.DMA((48,)),
+            pltpu.SemaphoreType.DMA,
         ],
         compiler_params=pltpu.CompilerParams(
             collective_id=0, has_side_effects=True, vmem_limit_bytes=56 * 1024 * 1024
@@ -526,7 +518,7 @@
         local_tiles,
         local_src,
         local_dst,
-        local_count,
+        local_count.reshape(1, 1),
         halo_tiles,
         halo_src,
         halo_dst,
@@ -535,6 +527,18 @@
         mask_nodes,
         remask_nodes,
     )
+    rebuilt, node_error = pl.pallas_call(
+        finish_kernel,
+        out_shape=(
+            jax.ShapeDtypeStruct((8, BLK, BLK), BF16),
+            jax.ShapeDtypeStruct((8, BLK), F32),
+        ),
+        in_specs=[vmem, vmem],
+        out_specs=(far, far),
+        scratch_shapes=[pltpu.SemaphoreType.DMA((2,))],
+        compiler_params=pltpu.CompilerParams(vmem_limit_bytes=4 * 1024 * 1024),
+        name="finish",
+    )(rebuilt, node_error)
     return rebuilt.reshape(1024, BLK), node_error.reshape(1024)
 
 

time: 43.7 us -> 39.5 us (0.904)
  Pallas kernels: 40.9 us -> 38 us
  local copies, waits for them, and re-layouts: 1.3 us -> 0 us
    pallas_call x1, Pallas kernels: 40.9 us -> 37.3 us  [per_device(): pl.pallas_call(step_kernel, out_shape=(pltpu.VMEM((8, BLK, BLK), BF16), p...]
    unnamed x2 -> x0, local copies, waits for them, and re-layouts: 1.3 us -> none
    pallas_call x0 -> x1, Pallas kernels: none -> 0.72 us  [per_device(): pl.pallas_call(finish_kernel, out_shape=(jax.ShapeDtypeStruct((8, BLK, BL...]
where the time goes in v3:
time: 39.5 us; the launch traced here: 39.3 us
  Pallas kernels  38 us (96%)
  between operations  1.29 us (3%)
    pallas_call x1, Pallas kernels, per_device(): pl.pallas_call(step_kernel, out_shape=(pltpu.VMEM((8, BLK, BLK), BF16), p...  37.3 us

profile of v3, /device:TPU:1, one launch (start us, length us, event | category | flops | bytes accessed | tf_op | source)
XLA Modules:
  0.0 39.3 jit_solution(4069423057494145700)
XLA Ops:
  1.3 37.3 %step.1 = (bf16[8,128,128]{2,1,0:T(8,128)(2,1)S(1)}, f32[8,128]{1,0:T(8,128)S(1)}) custom-call(bf16[8,128,512]{2,1,0:T(8,128)(2,1)} %bitcast.10, bf16[512,512]{1,0:T(8,128)(2,1)} %enc_weight.1, f32[1,512]{1,0:T(1,128)} %bitcast.13, f32[1,512]{1,0:T(1,128)} %bitcast.14, bf16[512]{0:T(512)(128)(2,1)} %dec_token.1, bf16[512,128]{1,0:T(8,128)(2,1)} %dec_weight.1, ...), custom_call_target="tpu_custom_call" | custom-call | tf_op jit(solution)/shard_map/step/pallas_call | solution.py:452
  38.6 0.7 %finish.1 = (bf16[8,128,128]{2,1,0:T(8,128)(2,1)}, f32[8,128]{1,0:T(8,128)}) custom-call(bf16[8,128,128]{2,1,0:T(8,128)(2,1)S(1)} %get-tuple-element.6.rebuilt, f32[8,128]{1,0:T(8,128)S(1)} %get-tuple-element.7.node_error), custom_call_target="tpu_custom_call" | custom-call | tf_op jit(solution)/shard_map/finish/pallas_call | solution.py:530

commit v4 on v3

--- a/solution.py
+++ b/solution.py
@@ -13,6 +13,18 @@
 FAR_8 = (4, 3, 5, 2, 6, 1, 7, 0)
 FAR_DOM = tuple((x, z) for x in FAR_X for z in FAR_8 if x or z)
 FAR_GROUP = tuple((y, c) for y in FAR_8 for c in (1, 0) if y or c)
+
+
+def hops(entry):
+    kind, a, b = entry
+    if kind == 0:
+        return min(a, 4 - a) + min(b, 8 - b)
+    return min(a, 8 - a)
+
+
+GREET = sorted(
+    [(0, x, z) for x, z in FAR_DOM] + [(1, y, c) for y, c in FAR_GROUP], key=hops, reverse=True
+)
 
 
 def iota(shape, axis):
@@ -91,6 +103,7 @@
     mz = md % 8
     my = mg // 2
     mc = mg % 2
+    mc_y = my % 2
     mq = mg // 4
 
     def turn(at, by, size):
@@ -135,26 +148,20 @@
         name: pltpu.make_async_copy(src, dst, load_sem.at[k])
         for k, (name, (src, dst)) in enumerate(zip(names, pairs))
     }
-    for name in names:
+    for name in names[:4]:
         loads[name].start()
 
     barrier = pltpu.get_barrier_semaphore()
 
     with jax.named_scope("greet"):
-        for x, z in FAR_DOM:
+        for kind, a, b in GREET:
+            device = (mg, dom_at(a, b)) if kind == 0 else (group_at(a, b), md)
             pl.semaphore_signal(
-                barrier,
-                inc=1,
-                device_id=(mg, dom_at(x, z)),
-                device_id_type=pl.DeviceIdType.MESH,
+                barrier, inc=1, device_id=device, device_id_type=pl.DeviceIdType.MESH
             )
-        for y, c in FAR_GROUP:
-            pl.semaphore_signal(
-                barrier,
-                inc=1,
-                device_id=(group_at(y, c), md),
-                device_id_type=pl.DeviceIdType.MESH,
-            )
+
+    for name in names[4:]:
+        loads[name].start()
 
     def set_rows(row, count, column):
         for j in range(8):
@@ -248,24 +255,43 @@
             device_id_type=pl.DeviceIdType.MESH,
         ).wait_send()
 
-    def gather_all(c, carry):
-        at = pl.ds(pl.multiple_of(c * 512, 512), 512)
-        rows = jnp.dot(onehot[at], enc[...].reshape(1024, 512), preferred_element_type=F32)
-        out_wide[at] = rows.astype(BF16)
-        return carry
+    pair = my + 1 - 2 * mc_y
+
+    def push(dom_ends, group_ends, x):
+        groups = [qs[x] * 4 + k for k in range(4)]
+        if x == 0:
+            groups = [pair * 2, pair * 2 + 1, my * 2 + cs[1]]
+        for k in range(4):
+            if k < len(groups):
+                group_copy(*group_ends, groups[k]).start()
+            for z in FAR_8[2 * k : 2 * k + 2]:
+                if x or z:
+                    dom_copy(*dom_ends, dom_at(x, z)).start()
+
+    def quarter(x):
+        upper = pl.ds(pl.multiple_of(xs[x] * BLK, BLK), BLK)
+        lower = pl.ds(pl.multiple_of((4 + qs[x]) * BLK, BLK), BLK)
+        return upper, lower
+
+    def gather_wide(x):
+        upper, lower = quarter(x)
+        chosen = jnp.concatenate([onehot[upper], onehot[lower]], axis=0)
+        rows = jnp.dot(chosen, enc[...].reshape(1024, 512), preferred_element_type=F32)
+        rows = rows.astype(BF16)
+        out_wide[upper] = rows[:BLK]
+        out_wide[lower] = rows[BLK:]
 
     with jax.named_scope("gather_wide"):
-        lax.fori_loop(0, 2, gather_all, 0)
+        gather_wide(FAR_X[0])
 
     with jax.named_scope("barrier"):
         pl.semaphore_wait(barrier, 46)
 
     with jax.named_scope("push"):
-        for k in range(16):
-            if k < 15:
-                group_copy(*wide_group, group_at(*FAR_GROUP[k])).start()
-            for x, z in FAR_DOM[2 * k : 2 * k + 2]:
-                dom_copy(*wide_dom, dom_at(x, z)).start()
+        for k in range(4):
+            push(wide_dom, wide_group, FAR_X[k])
+            if k < 3:
+                gather_wide(FAR_X[k + 1])
         keep_own(out_wide, in_wide)
 
     with jax.named_scope("chain"):
@@ -353,34 +379,28 @@
     with jax.named_scope("decode"):
         for n in range(8):
             summed = slots[final_s[n]]
-            latent = jnp.where(summed > 0, summed, slope_v[...] * summed)
+            latent = jnp.maximum(summed, slope_v[...] * summed)
             again = jnp.concatenate([remasked[n]] * 4, axis=1) > 0.5
             decoder_in = jnp.where(again, token, latent).astype(BF16)
             narrowed[n] = jnp.dot(decoder_in, decw_v[...], preferred_element_type=F32).astype(BF16)
 
     with jax.named_scope("gather_thin"):
+        waiting = None
         for x in FAR_X:
-            q = qs[x]
-            upper = pl.ds(pl.multiple_of(xs[x] * BLK, BLK), BLK)
-            lower = pl.ds(pl.multiple_of((4 + q) * BLK, BLK), BLK)
-            chosen = jnp.concatenate([onehot[upper], onehot[lower]], axis=0)
-            rows = jnp.dot(chosen, narrowed[...].reshape(1024, BLK), preferred_element_type=F32)
-            rows = rows.astype(BF16)
-            out_thin[upper] = rows[:BLK]
-            out_thin[lower] = rows[BLK:]
-            for k in range(4):
-                for z in FAR_8[2 * k : 2 * k + 2]:
-                    if x or z:
-                        dom_copy(*thin, dom_at(x, z)).start()
-                g = q * 4 + k
-                if x:
-                    group_copy(*thin, g).start()
-                else:
-
-                    @pl.when(g != mg)
-                    def _(g=g):
-                        group_copy(*thin, g).start()
-
+            upper, lower = quarter(x)
+            whole = narrowed[...].reshape(1024, BLK)
+            rows = [
+                jnp.dot(onehot[span], whole, preferred_element_type=F32) for span in (upper, lower)
+            ]
+            if waiting is not None:
+                push(thin, thin, waiting)
+            for span, made in zip((upper, lower), rows):
+                out_thin[span] = made.astype(BF16)
+            waiting = x
+            if x == FAR_X[0]:
+                push(thin, thin, x)
+                waiting = None
+        push(thin, thin, waiting)
         keep_own(out_thin, in_thin)
     with jax.named_scope("local_thin"):
         spread_local(narrowed, slots_thin)

time: 39.5 us -> 39.2 us (level)
  no operation moved by 1% of the time
where the time goes in v4:
time: 39.2 us; the launch traced here: 39.1 us
  Pallas kernels  37.8 us (96%)
  between operations  1.29 us (3%)
    pallas_call x1, Pallas kernels, per_device(): pl.pallas_call(step_kernel, out_shape=(pltpu.VMEM((8, BLK, BLK), BF16), p...  37.1 us

profile of v4, /device:TPU:1, one launch (start us, length us, event | category | flops | bytes accessed | tf_op | source)
XLA Modules:
  0.0 39.1 jit_solution(2771306344347122686)
XLA Ops:
  1.3 37.1 %step.1 = (bf16[8,128,128]{2,1,0:T(8,128)(2,1)S(1)}, f32[8,128]{1,0:T(8,128)S(1)}) custom-call(bf16[8,128,512]{2,1,0:T(8,128)(2,1)} %bitcast.10, bf16[512,512]{1,0:T(8,128)(2,1)} %enc_weight.1, f32[1,512]{1,0:T(1,128)} %bitcast.13, f32[1,512]{1,0:T(1,128)} %bitcast.14, bf16[512]{0:T(512)(128)(2,1)} %dec_token.1, bf16[512,128]{1,0:T(8,128)(2,1)} %dec_weight.1, ...), custom_call_target="tpu_custom_call" | custom-call | tf_op jit(solution)/shard_map/step/pallas_call | solution.py:472
  38.4 0.7 %finish.1 = (bf16[8,128,128]{2,1,0:T(8,128)(2,1)}, f32[8,128]{1,0:T(8,128)}) custom-call(bf16[8,128,128]{2,1,0:T(8,128)(2,1)S(1)} %get-tuple-element.6.rebuilt, f32[8,128]{1,0:T(8,128)S(1)} %get-tuple-element.7.node_error), custom_call_target="tpu_custom_call" | custom-call | tf_op jit(solution)/shard_map/finish/pallas_call | solution.py:550

commit v5 on v4

--- a/solution.py
+++ b/solution.py
@@ -29,6 +29,12 @@
 
 def iota(shape, axis):
     return lax.broadcasted_iota(I32, shape, axis)
+
+
+def row_sums(values):
+    column = jnp.sum(values, axis=1, keepdims=True)
+    on = iota((BLK, BLK), 0) == iota((BLK, BLK), 1)
+    return jnp.sum(jnp.where(on, column, 0.0), axis=0, keepdims=True)
 
 
 def step_kernel(
@@ -52,7 +58,9 @@
     mask_nodes,
     remask_nodes,
     rebuilt,
-    node_error,
+    tgt_v,
+    norms,
+    masked,
     hid_v,
     encw_v,
     bias_v,
@@ -60,7 +68,6 @@
     token_v,
     decw_v,
     dbias_v,
-    tgt_v,
     lt_v,
     lsrc_s,
     ldst_s,
@@ -79,10 +86,6 @@
     in_wide,
     slots,
     remasked,
-    masked,
-    norms,
-    dots,
-    powers,
     narrowed,
     out_thin,
     in_thin,
@@ -216,7 +219,8 @@
 
     wide_dom = (out_wide, in_wide, send_wide, recv_wide.at[mx])
     wide_group = (out_wide, in_wide, send_wide, recv_wide.at[4 + mq])
-    thin = (out_thin, in_thin, send_thin, recv_thin)
+    thin_dom = (out_thin, in_thin, send_thin, recv_thin.at[0])
+    thin_group = (out_thin, in_thin, send_thin, recv_thin.at[1])
 
     def keep_own(out_ref, in_ref):
         own = pl.ds(pl.multiple_of(md * 16, 16), 16)
@@ -283,6 +287,7 @@
 
     with jax.named_scope("gather_wide"):
         gather_wide(FAR_X[0])
+        gather_wide(FAR_X[1])
 
     with jax.named_scope("barrier"):
         pl.semaphore_wait(barrier, 46)
@@ -290,8 +295,8 @@
     with jax.named_scope("push"):
         for k in range(4):
             push(wide_dom, wide_group, FAR_X[k])
-            if k < 3:
-                gather_wide(FAR_X[k + 1])
+            if k < 2:
+                gather_wide(FAR_X[k + 2])
         keep_own(out_wide, in_wide)
 
     with jax.named_scope("chain"):
@@ -335,11 +340,6 @@
                 hit = jnp.where(column == iota((BLK, BLK), 1) + n * BLK, 1.0, 0.0)
                 masked[n : n + 1] += jnp.sum(hit, axis=0, keepdims=True)
 
-    def row_sums(values):
-        column = jnp.sum(values, axis=1, keepdims=True)
-        on = iota((BLK, BLK), 0) == iota((BLK, BLK), 1)
-        return jnp.sum(jnp.where(on, column, 0.0), axis=0, keepdims=True)
-
     with jax.named_scope("norms"):
         for name in ("bias", "tiles", "tgt", "halo", "slope", "token", "decw", "dbias"):
             loads[name].wait()
@@ -393,57 +393,64 @@
                 jnp.dot(onehot[span], whole, preferred_element_type=F32) for span in (upper, lower)
             ]
             if waiting is not None:
-                push(thin, thin, waiting)
+                push(thin_dom, thin_group, waiting)
             for span, made in zip((upper, lower), rows):
                 out_thin[span] = made.astype(BF16)
             waiting = x
             if x == FAR_X[0]:
-                push(thin, thin, x)
+                push(thin_dom, thin_group, x)
                 waiting = None
-        push(thin, thin, waiting)
+        push(thin_dom, thin_group, waiting)
         keep_own(out_thin, in_thin)
     with jax.named_scope("local_thin"):
         spread_local(narrowed, slots_thin)
         drain(out_wide, send_wide, recv_wide.at[0])
+    def halo_thin(half):
+        for c, off in enumerate((2, 3, 1, 0)):
+            b = 4 + qs[off] if half else xs[off]
+            rows = in_thin[pl.ds(pl.multiple_of(b * BLK, BLK), BLK)]
+            j = 2 * c + half
+            products[j] = jnp.dot(ht_v[tile_s[j]], rows, preferred_element_type=F32)
+
+    with jax.named_scope("await_group"):
+        await_rows(in_thin, 480, send_thin, recv_thin.at[1])
+        halo_thin(1)
     with jax.named_scope("await_thin"):
-        await_rows(in_thin, 976, send_thin, recv_thin)
+        await_rows(in_thin, 496, send_thin, recv_thin.at[0])
     with jax.named_scope("halo_thin"):
-        for c, off in enumerate((2, 3, 1, 0)):
-            for j, b in ((2 * c, xs[off]), (2 * c + 1, 4 + qs[off])):
-                rows = in_thin[pl.ds(pl.multiple_of(b * BLK, BLK), BLK)]
-                products[j] = jnp.dot(ht_v[tile_s[j]], rows, preferred_element_type=F32)
+        halo_thin(0)
         for j in range(8):
             slots_thin[20 + j] = slots_thin[prev_s[12 + j]] + products[j]
 
     with jax.named_scope("errors"):
         for n in range(8):
-            made = slots_thin[final_s[n]].astype(BF16)
-            rebuilt[n] = made
-            u = made.astype(F32)
-            x = tgt_v[n].astype(F32)
-            dots[n : n + 1] = row_sums(u * x)
-            powers[n : n + 1] = row_sums(u * u)
-        cosine = (
-            dots[...]
-            * (1.0 / BLK)
-            * lax.rsqrt(powers[...] * (1.0 / BLK) + 1e-06)
-            * lax.rsqrt(norms[...] * (1.0 / BLK) + 1e-06)
-        )
-        node_error[...] = jnp.where(masked[...] > 0.5, (1.0 - cosine) ** 2, 0.0)
+            rebuilt[n] = slots_thin[final_s[n]].astype(BF16)
 
     with jax.named_scope("drain"):
-        drain(out_thin, send_thin, recv_thin)
-
-
-def finish_kernel(rebuilt, node_error, rebuilt_out, node_error_out, sem):
-    copies = (
-        pltpu.make_async_copy(rebuilt, rebuilt_out, sem.at[0]),
-        pltpu.make_async_copy(node_error, node_error_out, sem.at[1]),
+        drain(out_thin, send_thin, recv_thin.at[0])
+
+
+def finish_kernel(
+    rebuilt, targets, norms, masked, rebuilt_out, node_error_out, dots, powers, node_error, sem
+):
+    values_copy = pltpu.make_async_copy(rebuilt, rebuilt_out, sem.at[0])
+    error_copy = pltpu.make_async_copy(node_error, node_error_out, sem.at[1])
+    values_copy.start()
+    for n in range(8):
+        u = rebuilt[n].astype(F32)
+        x = targets[n].astype(F32)
+        dots[n : n + 1] = row_sums(u * x)
+        powers[n : n + 1] = row_sums(u * u)
+    cosine = (
+        dots[...]
+        * (1.0 / BLK)
+        * lax.rsqrt(powers[...] * (1.0 / BLK) + 1e-06)
+        * lax.rsqrt(norms[...] * (1.0 / BLK) + 1e-06)
     )
-    for copy in copies:
-        copy.start()
-    for copy in copies:
-        copy.wait()
+    node_error[...] = jnp.where(masked[...] > 0.5, (1.0 - cosine) ** 2, 0.0)
+    error_copy.start()
+    values_copy.wait()
+    error_copy.wait()
 
 
 def per_device(
@@ -469,14 +476,16 @@
 ):
     vmem = pl.BlockSpec(memory_space=pltpu.VMEM)
     far = pl.BlockSpec(memory_space=pl.ANY)
-    rebuilt, node_error = pl.pallas_call(
+    made = pl.pallas_call(
         step_kernel,
         out_shape=(
             pltpu.VMEM((8, BLK, BLK), BF16),
+            pltpu.VMEM((8, BLK, BLK), BF16),
+            pltpu.VMEM((8, BLK), F32),
             pltpu.VMEM((8, BLK), F32),
         ),
         in_specs=[far] * 19,
-        out_specs=(vmem, vmem),
+        out_specs=(vmem,) * 4,
         scratch_shapes=[
             pltpu.VMEM((8, BLK, 512), BF16),
             pltpu.VMEM((512, 512), BF16),
@@ -485,7 +494,6 @@
             pltpu.VMEM((512,), BF16),
             pltpu.VMEM((512, BLK), BF16),
             pltpu.VMEM((1, BLK), F32),
-            pltpu.VMEM((8, BLK, BLK), BF16),
             pltpu.VMEM((12, BLK, BLK), BF16),
             pltpu.SMEM((1, 12), I32),
             pltpu.SMEM((1, 12), I32),
@@ -504,10 +512,6 @@
             pltpu.VMEM((1024, 512), BF16),
             pltpu.VMEM((28, BLK, 512), F32),
             pltpu.VMEM((8, BLK, BLK), F32),
-            pltpu.VMEM((8, BLK), F32),
-            pltpu.VMEM((8, BLK), F32),
-            pltpu.VMEM((8, BLK), F32),
-            pltpu.VMEM((8, BLK), F32),
             pltpu.VMEM((8, BLK, BLK), BF16),
             pltpu.VMEM((1024, BLK), BF16),
             pltpu.VMEM((1024, BLK), BF16),
@@ -520,7 +524,7 @@
             pltpu.SemaphoreType.DMA,
             pltpu.SemaphoreType.DMA((8,)),
             pltpu.SemaphoreType.DMA,
-            pltpu.SemaphoreType.DMA,
+            pltpu.SemaphoreType.DMA((2,)),
         ],
         compiler_params=pltpu.CompilerParams(
             collective_id=0, has_side_effects=True, vmem_limit_bytes=56 * 1024 * 1024
@@ -553,12 +557,17 @@
             jax.ShapeDtypeStruct((8, BLK, BLK), BF16),
             jax.ShapeDtypeStruct((8, BLK), F32),
         ),
-        in_specs=[vmem, vmem],
+        in_specs=[vmem] * 4,
         out_specs=(far, far),
-        scratch_shapes=[pltpu.SemaphoreType.DMA((2,))],
+        scratch_shapes=[
+            pltpu.VMEM((8, BLK), F32),
+            pltpu.VMEM((8, BLK), F32),
+            pltpu.VMEM((8, BLK), F32),
+            pltpu.SemaphoreType.DMA((2,)),
+        ],
         compiler_params=pltpu.CompilerParams(vmem_limit_bytes=4 * 1024 * 1024),
         name="finish",
-    )(rebuilt, node_error)
+    )(*made)
     return rebuilt.reshape(1024, BLK), node_error.reshape(1024)
 
 

time: 39.2 us -> 39.3 us (level)
  no operation moved by 1% of the time
where the time goes in v5:
time: 39.3 us; the launch traced here: 39.2 us
  Pallas kernels  37.9 us (96%)
  between operations  1.29 us (3%)
    pallas_call x1, Pallas kernels, per_device(): pl.pallas_call(step_kernel, out_shape=(pltpu.VMEM((8, BLK, BLK), BF16), p...  36.9 us
    pallas_call x1, Pallas kernels, per_device(): pl.pallas_call(finish_kernel, out_shape=(jax.ShapeDtypeStruct((8, BLK, BL...  0.98 us

profile of v5, /device:TPU:1, one launch (start us, length us, event | category | flops | bytes accessed | tf_op | source)
XLA Modules:
  0.0 39.2 jit_solution(8292551545872688598)
XLA Ops:
  1.3 36.9 %step.1 = (bf16[8,128,128]{2,1,0:T(8,128)(2,1)S(1)}, bf16[8,128,128]{2,1,0:T(8,128)(2,1)S(1)}, f32[8,128]{1,0:T(8,128)S(1)}, f32[8,128]{1,0:T(8,128)S(1)}) custom-call(bf16[8,128,512]{2,1,0:T(8,128)(2,1)} %bitcast.10, bf16[512,512]{1,0:T(8,128)(2,1)} %enc_weight.1, f32[1,512]{1,0:T(1,128)} %bitcast.13, f32[1,512]{1,0:T(1,128)} %bitcast.14, ...), custom_call_target="tpu_custom_call" | custom-call | tf_op jit(solution)/shard_map/step/pallas_call | solution.py:479
  38.2 1.0 %finish.1 = (bf16[8,128,128]{2,1,0:T(8,128)(2,1)}, f32[8,128]{1,0:T(8,128)}) custom-call(bf16[8,128,128]{2,1,0:T(8,128)(2,1)S(1)} %get-tuple-element.8.rebuilt, bf16[8,128,128]{2,1,0:T(8,128)(2,1)S(1)} %get-tuple-element.9.targets, f32[8,128]{1,0:T(8,128)S(1)} %get-tuple-element.10.norms, f32[8,128]{1,0:T(8,128)S(1)} %get-tuple-element.11.masked), custom_call_target="tpu_custom_call" | custom-call | tf_op jit(solution)/shard_map/finish/pallas_call | solution.py:554
